TPU v7x, 512 devices: a whole 4x8x8 slice. The times are simulated.
512 devices in a mesh: panel: 32 (over y_lo, z, core), rhs: 16 (over x, y_hi).
Axes of the slice: x: 4, y: 8 (y_hi: 4, y_lo: 2; y = y_hi * 2 + y_lo), z: 8, core: 2. Of those that a mesh axis runs over, the one named last changes fastest.
Arguments:
- pivot_rhs: float32 [2, 2048, 2048], P(None, 'panel', 'rhs'), may hold values from -6 to 6
- update_rhs: float32 [4096, 2048], P('panel', 'rhs'), may hold values from -6 to 6
- parent_rhs: float32 [4096, 2048], P('panel', 'rhs'), may hold values from -6 to 6
- lower_pivot: bfloat16 [2, 2048, 2048], P(None, 'panel', 'rhs'), may hold values from -1 to 1.4, as said below
- lower_update: bfloat16 [4096, 2048], P('panel', 'rhs'), may hold values from -0.125 to 0.125
- parent_lower: bfloat16 [4096, 4096], P('panel', 'rhs'), may hold values from -1 to 1.4, as said below
- parent_upper: bfloat16 [4096, 4096], P('panel', 'rhs'), may hold values from -1 to 1.4, as said below
- upper_pivot: bfloat16 [2, 2048, 2048], P(None, 'panel', 'rhs'), may hold values from -1 to 1.4, as said below
- upper_update: bfloat16 [2, 2048, 2048], P(None, 'panel', 'rhs'), may hold values from -0.125 to 0.125
- maps: int32 [4096], replicated, may hold values from 0 to 4095, as said below
Outputs:
- parent_solution: float32 [4096, 2048], P('panel', 'rhs')
- child_solution: float32 [2, 2048, 2048], P(None, 'panel', 'rhs')
Inputs may be any that keep to these rules, and one draw needn't show every extreme that they name: `maps`: for each child k, entry k * 2048 + i is 2 * i + b with b equal to 0 or 1; both values of b occur for each child in every draw. `lower_pivot`: each block is lower triangular, diagonal 0.6 to 1.4. `upper_pivot`: each block is upper triangular, diagonal 0.6 to 1.4. `parent_lower`: lower triangular, diagonal 0.6 to 1.4. `parent_upper`: upper triangular, diagonal 0.6 to 1.4.
All inputs are finite; a program needn't handle non-finite values.
Results may differ from a plain program's by a relative error of at most 0.0054.
Values may be sent and summed in bfloat16 or wider, within the bound.
A program may use at most 64 MiB of HBM per device.

v0:
```python
import functools

import jax
import jax.numpy as jnp
from jax import lax
from jax.experimental import pallas as pl
from jax.experimental.pallas import tpu as pltpu
from jax.sharding import PartitionSpec as P

BF = jnp.bfloat16
F32 = jnp.float32
MESH = pl.DeviceIdType.MESH


def dot(left, right):
    return jnp.dot(left, right, preferred_element_type=F32)


def kernel(
    panels,
    cols,
    pivot_rhs,
    update_rhs,
    parent_rhs,
    lower_pivot,
    lower_update,
    parent_lower,
    parent_upper,
    upper_pivot,
    upper_update,
    row_map,
    col_map,
    parent_out,
    child_out,
    pin,
    phalf,
    vec,
    x_pin,
    x_half,
    x_par,
    s_up,
    r_up,
    s_piv,
    r_piv,
    s_par,
    r_par,
    s_ch,
    r_ch,
    uhalf,
    moved,
    picked,
    direct,
    par_sum,
    spread_sum,
    child_sum,
    g_send,
    g_recv,
    f_send,
    rs_send,
    rs_recv,
    sh_send,
    sh_recv,
):
    me_p, me_r = lax.axis_index("panel"), lax.axis_index("rhs")
    total = panels * cols
    me = me_p * cols + me_r
    core = lax.rem(me_p, 2)
    mate = me_p + 1 - 2 * core
    per = panels // cols
    half = panels // 2
    m = parent_rhs.shape[0]
    mk = pivot_rhs.shape[1]
    child = me_p // half

    barrier = pltpu.get_barrier_semaphore()

    @pl.loop(1, total)
    def _(step):
        other = lax.rem(me + step, total)
        pl.semaphore_signal(
            barrier,
            inc=1,
            device_id=(other // cols, lax.rem(other, cols)),
            device_id_type=MESH,
        )

    pin[...] = pivot_rhs[...].astype(BF)
    direct[...] = jnp.zeros_like(direct)
    pl.semaphore_wait(barrier, total - 1)

    group = me_p // per
    last = cols - 1

    def every(source, goal):
        return None

    def below(source, goal):
        return goal >= source

    def above(source, goal):
        return goal <= source

    def guard(condition, action):
        if condition is None:
            action()
        else:
            pl.when(condition)(action)

    def both(first, second):
        return second if first is None else jnp.logical_and(first, second)

    def spot(buffer, depth, column, part, lead):
        rows = pl.ds(pl.multiple_of(part * depth, depth), depth)
        return buffer.at[column, slice(None) if lead is None else pl.ds(lead, 1), rows, :]

    class Gather:
        def __init__(self, stage, block, buffer, depth, keep, lead):
            self.stage, self.block, self.buffer, self.depth = stage, block, buffer, depth
            self.keep, self.lead = keep, lead
            self.active = keep(me_r, group)

        def place(self, column, part, panel):
            return spot(self.buffer, self.depth, column, part, self.lead(panel))

        def piece(self, panel):
            lead = self.lead(panel)
            return self.block if lead is None else self.block.at[pl.ds(lead, 1)]

        def goal(self, step):
            return lax.rem(me_p // 2 + step, half) * 2 + core

        def copy(self, step):
            goal = self.goal(step)
            return pltpu.make_async_remote_copy(
                src_ref=self.piece(goal),
                dst_ref=self.place(me_r, lax.rem(me_p, per), goal),
                send_sem=g_send.at[self.stage, step],
                recv_sem=g_recv.at[self.stage, me_r, lax.rem(me_p, per)],
                device_id=(goal, group),
                device_id_type=MESH,
            )

        def sends(self, action):
            for step in list(range(1, half)) + [0]:
                condition = self.keep(group, self.goal(step) // per)
                if step == 0:
                    condition = both(condition, group != me_r)
                guard(condition, functools.partial(action, step))

        def start(self):
            self.sends(lambda step: self.copy(step).start())

            @pl.when(group == me_r)
            def _():
                part = lax.rem(me_p, per)
                pltpu.make_async_copy(
                    self.piece(me_p),
                    self.place(me_r, part, me_p),
                    g_recv.at[self.stage, me_r, part],
                ).start()

        def landed(self, column, part):
            place = self.place(column, part, me_p)
            pltpu.make_async_copy(place, place, g_recv.at[self.stage, column, part]).wait()

        def forward(self, step, pair):
            column = lax.rem(me_r + 1 + step, cols)
            part = 2 * pair + core
            return pltpu.make_async_remote_copy(
                src_ref=self.place(column, part, me_p),
                dst_ref=self.place(column, part, me_p),
                send_sem=f_send.at[self.stage, step, pair],
                recv_sem=g_recv.at[self.stage, column, part],
                device_id=(mate, me_r),
                device_id_type=MESH,
            )

        def pass_on(self):
            def action():
                for step in [last] + list(range(last)):
                    for pair in range(per // 2):
                        self.landed(lax.rem(me_r + 1 + step, cols), 2 * pair + core)
                        self.forward(step, pair).start()

            guard(self.active, action)

        def arrive(self, step):
            column = lax.rem(me_r + 1 + step, cols)
            for pair in range(per // 2):
                self.landed(column, 2 * pair + 1 - core)
            return column

        def finish(self):
            self.sends(lambda step: self.copy(step).wait_send())

            def action():
                for step in range(cols):
                    for pair in range(per // 2):
                        self.forward(step, pair).wait_send()

            guard(self.active, action)

    class Scatter:
        def __init__(self, stage, source, target, keep):
            self.stage, self.source, self.target, self.keep = stage, source, target, keep
            self.active = keep(me_r, group)

        def copy(self, step):
            return pltpu.make_async_remote_copy(
                src_ref=self.source.at[step],
                dst_ref=self.target.at[step],
                send_sem=rs_send.at[self.stage, step],
                recv_sem=rs_recv.at[self.stage, step],
                device_id=(me_p, lax.rem(me_r + 1 + step, cols)),
                device_id_type=MESH,
            )

        def add(self, total_ref):
            for step in range(last):
                sender = lax.rem(me_r + last - step, cols)

                def action(step=step):
                    self.copy(step).wait_recv()
                    total_ref[...] += self.target[step].astype(F32)

                guard(self.keep(sender, group), action)

        def finish(self):
            def action():
                for step in range(last):
                    self.copy(step).wait_send()

            guard(self.active, action)

    def targets(ref, k, index, size, base):
        if ref.shape[0] == 2:
            return ref[k : k + 1, :]
        start = pl.multiple_of(k * (ref.shape[1] // 2) + index * size, 128)
        return ref[:, pl.ds(start, size)] - base

    def whole(panel):
        return None

    def same(panel):
        return panel // half

    def other(panel):
        return 1 - panel // half

    g_own = Gather(0, pin, x_pin, mk, every, same)
    g_other = Gather(5, pin, x_pin, mk, below, other)
    g_low = Gather(1, vec.at[0], x_par.at[0], m, below, whole)
    g_half = Gather(2, phalf, x_half, mk, above, whole)
    g_up = Gather(3, vec.at[1], x_par.at[1], m, above, whole)
    g_all = Gather(4, vec.at[2], x_par.at[2], m, every, whole)
    t_up = Scatter(0, s_up, r_up, every)
    t_piv = Scatter(1, s_piv, r_piv, below)
    t_low = Scatter(2, s_par.at[0], r_par.at[0], below)
    t_high = Scatter(3, s_par.at[1], r_par.at[1], above)
    t_child = Scatter(4, s_ch, r_ch, every)

    g_own.start()
    g_other.start()

    width = upper_update.shape[2]
    for k in range(2):
        rows = lax.broadcasted_iota(jnp.int32, (per * m, width), 0)
        chosen = (rows == targets(col_map, k, me_r, width, me_r * per * m)).astype(F32).astype(BF)
        picked[k] = lax.dot_general(
            upper_update[k], chosen, (((1,), (1,)), ((), ())), preferred_element_type=F32
        ).astype(BF)
    spread_sum[...] = parent_rhs[...]

    g_own.pass_on()
    for step in range(cols):
        column = g_own.arrive(step)
        value = dot(lower_update[...], x_pin[column, child])
        if step < last:
            s_up[step] = value.astype(BF)
            t_up.copy(step).start()
        else:
            par_sum[...] = update_rhs[...] + value
    g_other.pass_on()
    t_up.add(par_sum)
    update = par_sum[...].astype(BF)
    uhalf[0] = update[: m // 2]
    uhalf[1] = update[m // 2 :]
    first = lax.rem(me_p, half) * 2

    def shuffle(side):
        return pltpu.make_async_remote_copy(
            src_ref=uhalf.at[side],
            dst_ref=moved.at[child],
            send_sem=sh_send.at[side],
            recv_sem=sh_recv.at[child],
            device_id=(first + side, me_r),
            device_id_type=MESH,
        )

    for side in range(2):

        @pl.when(first + side != me_p)
        def _():
            shuffle(side).start()

        @pl.when(first + side == me_p)
        def _():
            pltpu.make_async_copy(uhalf.at[side], moved.at[child], sh_recv.at[child]).start()

    child_sum[...] = jnp.zeros_like(child_sum)

    def pivots():
        for step in range(cols):
            column = g_other.arrive(step)
            for k in range(2):
                value = dot(lower_pivot[k], x_pin[column, k])
                if step < last:
                    s_piv[step, k] = value.astype(BF)
                else:
                    child_sum[k] = value
            if step < last:
                t_piv.copy(step).start()

    guard(g_other.active, pivots)

    rows = lax.broadcasted_iota(jnp.int32, (m, m // 2), 0)
    for k in range(2):
        pltpu.make_async_copy(moved.at[k], moved.at[k], sh_recv.at[k]).wait()
        chosen = (rows == targets(row_map, k, me_p, m // 2, me_p * m)).astype(F32).astype(BF)
        spread_sum[...] += dot(chosen, moved[k])
    vec[0, 0] = spread_sum[...].astype(BF)
    g_low.start()

    t_piv.add(child_sum)
    phalf[...] = child_sum[...].astype(BF)
    g_half.start()

    def parent(level, gather, scatter, factor):
        par_sum[...] = jnp.zeros_like(par_sum)
        gather.pass_on()

        def action():
            for step in range(cols):
                column = gather.arrive(step)
                value = dot(factor[...], x_par[level, column, 0])
                if step < last:
                    s_par[level, step] = value.astype(BF)
                    scatter.copy(step).start()
                else:
                    par_sum[...] = value

        guard(gather.active, action)
        scatter.add(par_sum)
        vec[level + 1, 0] = par_sum[...].astype(BF)

    parent(0, g_low, t_low, parent_lower)
    g_up.start()
    g_half.pass_on()

    def known():
        for step in range(cols):
            column = g_half.arrive(step)
            for k in range(2):
                direct[step, k] = dot(upper_pivot[k], x_half[column, k])

    guard(g_half.active, known)
    parent(1, g_up, t_high, parent_upper)
    g_all.start()
    parent_out[...] = par_sum[...]

    g_all.pass_on()
    for step in range(cols):
        column = g_all.arrive(step)
        for k in range(2):
            value = direct[step, k] + dot(picked[k], x_par[2, column, 0])
            if step < last:
                s_ch[step, k] = value.astype(BF)
            else:
                child_out[k] = value
        if step < last:
            t_child.copy(step).start()
    for gather in (g_own, g_other, g_low, g_half, g_up, g_all):
        gather.finish()
    for side in range(2):

        @pl.when(first + side != me_p)
        def _():
            shuffle(side).wait_send()

    t_child.add(child_out)
    for scatter in (t_up, t_piv, t_low, t_high, t_child):
        scatter.finish()


def shards(panels, cols, *arguments):
    *arrays, maps = arguments
    m, width = arrays[1].shape
    mk = arrays[0].shape[1]
    per = panels // cols
    sides = maps.reshape(2, -1)
    me_p, me_r = lax.axis_index("panel"), lax.axis_index("rhs")
    wide = arrays[8].shape[2]

    def cut(index, size, base):
        if size % 128 == 0:
            return maps.reshape(1, -1)
        return lax.dynamic_slice_in_dim(sides, index * size, size, 1) - base

    row_map = cut(me_p, m // 2, me_p * m)
    col_map = cut(me_r, wide, me_r * per * m)
    vm = pltpu.VMEM
    dma = pltpu.SemaphoreType.DMA
    return pl.pallas_call(
        functools.partial(kernel, panels, cols),
        out_shape=(
            jax.ShapeDtypeStruct((m, width), F32),
            jax.ShapeDtypeStruct((2, mk, width), F32),
        ),
        in_specs=[pl.BlockSpec(memory_space=pltpu.VMEM)] * 11,
        out_specs=(pl.BlockSpec(memory_space=pltpu.VMEM),) * 2,
        scratch_shapes=[
            vm((2, mk, width), BF),
            vm((2, mk, width), BF),
            vm((3, 1, m, width), BF),
            vm((cols, 2, per * mk, width), BF),
            vm((cols, 2, per * mk, width), BF),
            vm((3, cols, 1, per * m, width), BF),
            vm((cols - 1, m, width), BF),
            vm((cols - 1, m, width), BF),
            vm((cols - 1, 2, mk, width), BF),
            vm((cols - 1, 2, mk, width), BF),
            vm((2, cols - 1, m, width), BF),
            vm((2, cols - 1, m, width), BF),
            vm((cols - 1, 2, mk, width), BF),
            vm((cols - 1, 2, mk, width), BF),
            vm((2, m // 2, width), BF),
            vm((2, m // 2, width), BF),
            vm((2, mk, per * m), BF),
            vm((cols, 2, mk, width), F32),
            vm((m, width), F32),
            vm((m, width), F32),
            vm((2, mk, width), F32),
            dma((6, panels // 2)),
            dma((6, cols, per)),
            dma((6, cols, per // 2)),
            dma((5, cols - 1)),
            dma((5, cols - 1)),
            dma((2,)),
            dma((2,)),
        ],
        compiler_params=pltpu.CompilerParams(
            collective_id=0, has_side_effects=True, vmem_limit_bytes=60 * 1024 * 1024
        ),
    )(*arrays, row_map, col_map)


def solution(mesh):
    panels, cols = mesh.shape["panel"], mesh.shape["rhs"]
    placed = (
        P(None, "panel", "rhs"),
        P("panel", "rhs"),
        P("panel", "rhs"),
        P(None, "panel", "rhs"),
        P("panel", "rhs"),
        P("panel", "rhs"),
        P("panel", "rhs"),
        P(None, "panel", "rhs"),
        P(None, "panel", "rhs"),
        P(),
    )
    return jax.shard_map(
        functools.partial(shards, panels, cols),
        mesh=mesh,
        in_specs=placed,
        out_specs=(P("panel", "rhs"), P(None, "panel", "rhs")),
        check_vma=False,
    )
```

profile of v0, /device:TPU:1, one launch (start us, length us, event | category | flops | bytes accessed | tf_op | source)
XLA Modules:
  0.0 237.3 jit_solution(15098948829888563386)
XLA Ops:
  0.6 0.0 copy-start.1
  0.6 0.7 copy-done.1
  1.4 0.6 dynamic-slice_subtract_fusion.row_map
  2.0 233.1 %shard_map.113 = (f32[128,128]{1,0:T(8,128)}, f32[2,64,128]{2,1,0:T(8,128)}) custom-call(f32[2,64,128]{2,1,0:T(8,128)} %pivot_rhs.1, f32[128,128]{1,0:T(8,128)} %update_rhs.1, f32[128,128]{1,0:T(8,128)} %parent_rhs.1, bf16[2,64,128]{2,1,0:T(8,128)(2,1)} %lower_pivot.1, bf16[128,128]{1,0:T(8,128)(2,1)} %lower_update.1, bf16[128,256]{1,0:T(8,128)(2,1)} %parent_lower.1, ...), custom_call_target="tpu_custom_call" | custom-call | tf_op jit(solution)/shard_map/pallas_call | solution.py:413
  235.1 0.0 copy-start
  235.1 1.5 copy.14
  236.6 0.0 copy-done
  236.6 0.6 copy.15
  (1 shorter events, 0.0 us)
Async XLA Ops:
  0.6 0.7 copy-start.1
  235.1 1.5 copy-start
where the time goes:
time: 238 us; the launch traced here: 237 us
  Pallas kernels  233 us (98%)
  local copies, waits for them, and re-layouts  2.86 us (1%)
    pallas_call x1, Pallas kernels, shards(): pl.pallas_call(functools.partial(kernel, panels, cols), out_shape=(jax.Sh...  233 us

commit v1 on v0

v1 whole, which is shorter than its diff:
```python
import functools

import jax
import jax.numpy as jnp
from jax import lax
from jax.experimental import pallas as pl
from jax.experimental.pallas import tpu as pltpu
from jax.sharding import PartitionSpec as P

BF = jnp.bfloat16
F32 = jnp.float32
MESH = pl.DeviceIdType.MESH

Z = 8
DIST = (0, -1, 1, -2, 2, -3, 3, 4)
N_GATHER, N_SPREAD = 5, 4
SENDS = 32


def dot(left, right):
    return jnp.dot(left, right, preferred_element_type=F32)


def kernel(
    pivot_rhs,
    update_rhs,
    parent_rhs,
    lower_pivot,
    lower_update,
    parent_lower,
    parent_upper,
    upper_pivot,
    upper_update,
    maps,
    parent_out,
    child_out,
    x_pin,
    x_half,
    x_sol,
    x_sum,
    x_mid,
    a_low,
    a_par,
    a_piv,
    a_up,
    moved_rhs,
    pick,
    acc,
    direct,
    g_send,
    g_recv,
    s_send,
    s_recv,
    e_send,
    e_recv,
    h_send,
    h_recv,
):
    me_p, me_r = lax.axis_index("panel"), lax.axis_index("rhs")
    core = lax.rem(me_p, 2)
    c = me_p // 2
    z, y_lo = lax.rem(c, Z), c // Z
    x, y_hi = me_r // 4, lax.rem(me_r, 4)
    mate_y = 1 - y_lo
    sib = me_p + 1 - 2 * core

    def chip(y, dist):
        return y * Z + lax.rem(z + dist + Z, Z)

    def at_z(dist):
        return chip(y_lo, dist) * 2 + core

    def at_xy(dx, dy):
        return lax.rem(x + dx + 4, 4) * 4 + lax.rem(y_hi + dy + 4, 4)

    across = (mate_y * Z + z) * 2 + core
    goal = lax.rem(me_p, 2 * Z) * 2

    barrier = pltpu.get_barrier_semaphore()
    friends = [(at_z(d), me_r) for d in (-1, 1, -2, 2)] + [(across, me_r), (sib, me_r)]
    friends += [(me_p, at_xy(*d)) for d in ((0, -1), (0, 1), (-1, 0), (1, 0))]
    for friend in friends:
        pl.semaphore_signal(barrier, inc=1, device_id=friend, device_id_type=MESH)
    for child in range(2):
        source = c + 2 * Z * child

        @pl.when(source != me_p)
        def _():
            pl.semaphore_signal(barrier, inc=1, device_id=(source, me_r), device_id_type=MESH)

    pending = []

    def rcopy(src, dst, send, recv, device):
        return pltpu.make_async_remote_copy(
            src_ref=src, dst_ref=dst, send_sem=send, recv_sem=recv, device_id=device, device_id_type=MESH
        )

    def send(src, dst, ssem, rsem, device, when=None):
        def go():
            rcopy(src, dst, ssem, rsem, device).start()

        def done():
            rcopy(src, dst, ssem, rsem, device).wait_send()

        pending.append((when, done))
        if when is None:
            go()
        else:
            pl.when(when)(go)

    def landed(ref, sem):
        pltpu.make_async_copy(ref, ref, sem).wait()

    class Gather:
        def __init__(self, g, place):
            self.g, self.place, self.n = g, place, 0

        def sem(self, side, col, dist):
            return g_recv.at[self.g, side * 16 + col * 8 + DIST.index(dist)]

        def block(self, col, dist, side=0):
            y = y_lo if col == 0 else mate_y
            return self.place(chip(y, dist), core if side == 0 else 1 - core)

        def put(self, col, dist, to, side, col_there, dist_there, when=None):
            ref = self.block(col, dist)
            send(
                ref,
                ref,
                g_send.at[self.g, self.n],
                self.sem(side, col_there, dist_there),
                (to, me_r),
                when,
            )
            self.n += 1

        def start(self):
            for d in (2, -2, 1, -1):
                self.put(0, 0, at_z(d), 0, 0, -d)
            self.put(0, 0, across, 0, 1, 0)
            self.put(0, 0, sib, 1, 0, 0)

        def hop(self, d):
            landed(self.block(0, d), self.sem(0, 0, d))
            if d == -2:
                self.put(0, d, at_z(1), 0, 0, -3)
                self.put(0, d, at_z(2), 0, 0, 4, core == 0)
            if d == 2:
                self.put(0, d, at_z(-1), 0, 0, 3)
                self.put(0, d, at_z(-2), 0, 0, 4, core == 1)
            self.put(0, d, across, 0, 1, d)
            self.put(0, d, sib, 1, 0, d)

        def over(self, d):
            landed(self.block(1, d), self.sem(0, 1, d))
            self.put(1, d, sib, 1, 1, d)

        def arrive(self, col, d):
            landed(self.block(col, d, 1), self.sem(1, col, d))

    class Spread:
        def __init__(self, a, place):
            self.a, self.place, self.n = a, place, 0

        def sem(self, hop, piece):
            return s_recv.at[self.a, hop * 4 + piece]

        def block(self, hop, piece):
            dx = {0: 0, 1: -1, 2: 1, 3: 2}[hop]
            dy = {0: 0, 1: -1, 2: 1, 3: 2}[piece]
            return self.place(at_xy(dx, dy))

        def put(self, hop, piece, to, hop_there, piece_there, when=None):
            ref = self.block(hop, piece)
            send(
                ref,
                ref,
                s_send.at[self.a, self.n],
                self.sem(hop_there, piece_there),
                (me_p, to),
                when,
            )
            self.n += 1

        def start(self):
            self.put(0, 0, at_xy(0, 1), 0, 1)
            self.put(0, 0, at_xy(0, -1), 0, 2)

        def wait(self, hop, piece):
            landed(self.block(hop, piece), self.sem(hop, piece))

        def turn(self):
            self.wait(0, 1)
            self.put(0, 1, at_xy(0, 1), 0, 3, core == 0)
            self.wait(0, 2)
            self.put(0, 2, at_xy(0, -1), 0, 3, core == 1)

        def out(self, piece):
            if piece == 3:
                self.wait(0, 3)
            self.put(0, piece, at_xy(1, 0), 1, piece)
            self.put(0, piece, at_xy(-1, 0), 2, piece)

        def on(self, piece):
            self.wait(1, piece)
            self.put(1, piece, at_xy(1, 0), 3, piece, core == 0)
            self.wait(2, piece)
            self.put(2, piece, at_xy(-1, 0), 3, piece, core == 1)

        def end(self):
            for piece in range(4):
                self.wait(3, piece)

    class Extra:
        def __init__(self, e, ref):
            self.e, self.ref = e, ref
            self.dx = lax.rem(x - c // 4 + 4, 4)
            self.dy = lax.rem(y_hi - lax.rem(c, 4) + 4, 4)
            self.n = 0

        def put(self, to, when):
            send(self.ref, self.ref, e_send.at[self.e, self.n], e_recv.at[self.e], (me_p, to), when)
            self.n += 1

        def wait(self, when):
            @pl.when(when)
            def _():
                landed(self.ref, e_recv.at[self.e])

        def both(self, *conditions):
            return functools.reduce(jnp.logical_and, conditions)

        def start(self):
            source = self.both(self.dx == 0, self.dy == 0)
            self.put(at_xy(0, 1), source)
            self.put(at_xy(0, -1), source)
            self.put(at_xy(1, 0), source)
            self.put(at_xy(-1, 0), source)

        def turn(self):
            low, high = self.both(self.dx == 0, self.dy == 1), self.both(self.dx == 0, self.dy == 3)
            near = self.both(self.dx == 0, lax.rem(self.dy, 2) == 1)
            self.wait(near)
            self.put(at_xy(0, 1), self.both(low, core == 0))
            self.put(at_xy(0, -1), self.both(high, core == 1))
            self.put(at_xy(1, 0), near)
            self.put(at_xy(-1, 0), near)

        def out(self):
            far = self.both(self.dx == 0, self.dy == 2)
            self.wait(far)
            self.put(at_xy(1, 0), far)
            self.put(at_xy(-1, 0), far)

        def on(self):
            self.wait(lax.rem(self.dx, 2) == 1)
            self.put(at_xy(1, 0), self.both(self.dx == 1, core == 0))
            self.put(at_xy(-1, 0), self.both(self.dx == 3, core == 1))

        def end(self):
            self.wait(self.dx == 2)

    def two(buffer):
        return lambda chip_at, core_at: buffer.at[:, chip_at, core_at]

    def one(buffer):
        return lambda chip_at, core_at: buffer.at[chip_at, core_at]

    def slot(r):
        return r + (r + 15 - c) // 16

    g_pin = Gather(0, two(x_pin))
    g_sum = Gather(1, one(x_sum))
    g_mid = Gather(2, one(x_mid))
    g_sol = Gather(3, two(x_sol))
    g_half = Gather(4, two(x_half))
    f_low = Spread(0, lambda r: a_low.at[r])
    f_par = Spread(1, lambda r: a_par.at[slot(r)])
    f_piv = Spread(2, lambda r: a_piv.at[slot(r)])
    f_up = Spread(3, lambda r: a_up.at[r])
    e_par = Extra(0, a_par.at[c + 1])
    e_piv = Extra(1, a_piv.at[c + 1])

    x_pin[:, c, core] = pivot_rhs[...].astype(BF)

    @pl.when(me_r <= c)
    def _():
        a_par[me_r] = parent_lower[...]
        a_piv[me_r] = lower_pivot[...]

    @pl.when(me_r >= c)
    def _():
        a_par[me_r + 1] = parent_upper[...]
        a_piv[me_r + 1] = upper_pivot[...]

    a_up[me_r] = upper_update[...]
    alone = (31 - me_p) // 31 + me_p // 31
    pl.semaphore_wait(barrier, len(friends) + 2 - alone)

    def shuffle(src, dst, n):
        for side in range(2):
            there = goal + side
            piece = src.at[pl.ds(side * 64, 64)]
            send(piece, dst, h_send.at[n, side], h_recv.at[n, y_lo], (there, me_r), there != me_p)

            @pl.when(there == me_p)
            def _():
                pltpu.make_async_copy(piece, dst, h_recv.at[n, y_lo]).start()

    shuffle(lower_update, a_low.at[me_r, y_lo], 0)
    g_pin.start()
    f_par.start()
    f_par.out(0)
    shuffle(update_rhs, moved_rhs.at[y_lo], 1)

    start = pl.multiple_of(c * 128, 128)
    lanes = [maps[:, pl.ds(k * 2048 + start, 128)] - me_p * 128 for k in range(2)]
    low = jnp.concatenate([lanes[0][:, :64], lanes[1][:, :64]], axis=1)
    high = jnp.concatenate([lanes[0][:, 64:], lanes[1][:, 64:]], axis=1)
    targets = jnp.where(core == 0, low, high)
    rows = lax.broadcasted_iota(jnp.int32, (128, 128), 0)
    chosen = (rows == targets).astype(F32)
    pick[0] = chosen.astype(BF)
    pick[1] = chosen.T.astype(BF)

    g_pin.hop(-2)
    g_pin.hop(2)
    g_pin.hop(-1)
    g_pin.hop(1)
    g_pin.over(0)
    for child in range(2):
        landed(a_low.at[me_r, child], h_recv.at[0, child])
    f_low.start()
    f_low.out(0)
    g_pin.over(-1)
    g_pin.over(1)
    for d in (-3, 3, 4):
        g_pin.hop(d)
    f_par.turn()
    f_par.out(1)
    f_par.out(2)
    f_low.turn()
    f_low.out(1)
    f_low.out(2)
    for d in (-2, 2, -3, 3, 4):
        g_pin.over(d)
    f_low.out(3)
    for piece in (0, 1, 2):
        f_low.on(piece)
    f_low.on(3)
    f_par.out(3)
    e_par.start()
    e_piv.start()
    for child in range(2):
        landed(moved_rhs.at[child], h_recv.at[1, child])
    for col in range(2):
        for d in DIST:
            g_pin.arrive(col, d)
    f_low.end()

    def blocks(buffer, k, r):
        return buffer[k, r].reshape(128, 128)

    halves = []
    for k in range(2):
        value = moved_rhs[k]
        for r in range(16):
            value += dot(a_low[r, k], blocks(x_pin, k, r))
        halves.append(value.astype(BF))
    total = parent_rhs[...] + dot(pick[0], jnp.concatenate(halves, axis=0))
    x_sum[c, core] = total.astype(BF)
    g_sum.start()

    f_piv.start()
    f_piv.out(0)
    f_up.start()
    f_par.on(0)
    g_sum.hop(-2)
    g_sum.hop(2)
    g_sum.hop(-1)
    g_sum.hop(1)
    f_par.on(1)
    f_par.on(2)
    g_sum.over(0)
    g_sum.over(-1)
    g_sum.over(1)
    for d in (-3, 3, 4):
        g_sum.hop(d)
    f_par.on(3)
    e_par.turn()
    for d in (-2, 2, -3, 3, 4):
        g_sum.over(d)
    f_par.end()
    for col in range(2):
        for d in DIST:
            g_sum.arrive(col, d)

    def pair(buffer, r):
        return buffer[r].reshape(256, 128)

    def lower(r):
        return r <= c

    def upper(r):
        return r >= c

    acc[...] = jnp.zeros_like(acc)
    for r in range(16):

        @pl.when(lower(r))
        def _():
            acc[...] += dot(a_par[r], pair(x_sum, r))

    x_mid[c, core] = acc[...].astype(BF)
    g_mid.start()

    f_piv.turn()
    f_piv.out(1)
    f_piv.out(2)
    f_up.out(0)
    g_mid.hop(-2)
    g_mid.hop(2)
    g_mid.hop(-1)
    g_mid.hop(1)
    f_up.turn()
    f_piv.out(3)
    e_par.out()
    e_piv.turn()
    g_mid.over(0)
    g_mid.over(-1)
    g_mid.over(1)
    for d in (-3, 3, 4):
        g_mid.hop(d)
    f_up.out(1)
    f_up.out(2)
    f_up.out(3)
    for piece in range(4):
        f_piv.on(piece)
    e_par.on()
    e_piv.out()
    for d in (-2, 2, -3, 3, 4):
        g_mid.over(d)
    f_piv.end()
    e_piv.on()

    direct[...] = jnp.zeros_like(direct)
    for r in range(16):

        @pl.when(lower(r))
        def _():
            for k in range(2):
                direct[k] += dot(a_piv[r, k], blocks(x_pin, k, r))

    x_half[:, c, core] = direct[...].astype(BF)
    g_half.start()
    for col in range(2):
        for d in DIST:
            g_mid.arrive(col, d)
    e_par.end()

    acc[...] = jnp.zeros_like(acc)
    for r in range(16):

        @pl.when(upper(r))
        def _():
            acc[...] += dot(a_par[r + 1], pair(x_mid, r))

    parent_out[...] = acc[...]
    picked = dot(pick[1], acc[...].astype(BF)).astype(BF)
    x_sol[:, c, core] = picked.reshape(2, 64, 128)
    g_sol.start()

    for d in (-2, 2, -1, 1):
        g_half.hop(d)
    g_half.over(0)
    for piece in range(4):
        f_up.on(piece)
    for d in (-2, 2, -1, 1):
        g_sol.hop(d)
    g_sol.over(0)
    g_sol.over(-1)
    g_sol.over(1)
    for d in (-3, 3, 4):
        g_half.hop(d)
    for d in (-3, 3, 4):
        g_sol.hop(d)
    for d in (-1, 1, -2, 2, -3, 3, 4):
        g_half.over(d)
    for d in (-2, 2, -3, 3, 4):
        g_sol.over(d)
    e_piv.end()
    for col in range(2):
        for d in DIST:
            g_half.arrive(col, d)

    direct[...] = jnp.zeros_like(direct)
    for r in range(16):

        @pl.when(upper(r))
        def _():
            for k in range(2):
                direct[k] += dot(a_piv[r + 1, k], blocks(x_half, k, r))

    f_up.end()
    for col in range(2):
        for d in DIST:
            g_sol.arrive(col, d)
    for k in range(2):
        value = direct[k]
        for r in range(16):
            value += dot(a_up[r, k], blocks(x_sol, k, r))
        child_out[k] = value

    for when, done in pending:
        if when is None:
            done()
        else:
            pl.when(when)(done)


def shards(*arguments):
    *arrays, maps = arguments
    vm = pltpu.VMEM
    dma = pltpu.SemaphoreType.DMA
    return pl.pallas_call(
        kernel,
        out_shape=(
            jax.ShapeDtypeStruct((128, 128), F32),
            jax.ShapeDtypeStruct((2, 64, 128), F32),
        ),
        in_specs=[pl.BlockSpec(memory_space=pltpu.VMEM)] * 10,
        out_specs=(pl.BlockSpec(memory_space=pltpu.VMEM),) * 2,
        scratch_shapes=[
            vm((2, 16, 2, 64, 128), BF),
            vm((2, 16, 2, 64, 128), BF),
            vm((2, 16, 2, 64, 128), BF),
            vm((16, 2, 128, 128), BF),
            vm((16, 2, 128, 128), BF),
            vm((16, 2, 64, 128), BF),
            vm((17, 128, 256), BF),
            vm((17, 2, 64, 128), BF),
            vm((16, 2, 64, 128), BF),
            vm((2, 64, 128), F32),
            vm((2, 128, 128), BF),
            vm((128, 128), F32),
            vm((2, 64, 128), F32),
            dma((N_GATHER, SENDS)),
            dma((N_GATHER, 32)),
            dma((N_SPREAD, 20)),
            dma((N_SPREAD, 16)),
            dma((2, 12)),
            dma((2,)),
            dma((2, 2)),
            dma((2, 2)),
        ],
        compiler_params=pltpu.CompilerParams(
            collective_id=0, has_side_effects=True, vmem_limit_bytes=60 * 1024 * 1024
        ),
    )(*arrays, maps.reshape(1, -1))


def solution(mesh):
    placed = (
        P(None, "panel", "rhs"),
        P("panel", "rhs"),
        P("panel", "rhs"),
        P(None, "panel", "rhs"),
        P("panel", "rhs"),
        P("panel", "rhs"),
        P("panel", "rhs"),
        P(None, "panel", "rhs"),
        P(None, "panel", "rhs"),
        P(),
    )
    return jax.shard_map(
        shards,
        mesh=mesh,
        in_specs=placed,
        out_specs=(P("panel", "rhs"), P(None, "panel", "rhs")),
        check_vma=False,
    )
```

time: 238 us -> 97.6 us (0.41)
  Pallas kernels: 233 us -> 94.6 us
    pallas_call x1, Pallas kernels: 233 us -> 94.6 us  [shards(): pl.pallas_call(kernel, out_shape=(jax.ShapeDtypeStruct((128, 128), F32),...]
where the time goes in v1:
time: 97.6 us; the launch traced here: 97.4 us
  Pallas kernels  94.6 us (97%)
  local copies, waits for them, and re-layouts  2.14 us (2%)
    pallas_call x1, Pallas kernels, shards(): pl.pallas_call(kernel, out_shape=(jax.ShapeDtypeStruct((128, 128), F32),...  94.6 us
    unnamed x4, local copies, waits for them, and re-layouts  2.14 us

profile of v1, /device:TPU:1, one launch (start us, length us, event | category | flops | bytes accessed | tf_op | source)
XLA Modules:
  0.0 97.4 jit_solution(6910498881092822125)
XLA Ops:
  0.6 94.6 %shard_map.113 = (f32[128,128]{1,0:T(8,128)}, f32[2,64,128]{2,1,0:T(8,128)}) custom-call(f32[2,64,128]{2,1,0:T(8,128)} %pivot_rhs.1, f32[128,128]{1,0:T(8,128)} %update_rhs.1, f32[128,128]{1,0:T(8,128)} %parent_rhs.1, bf16[2,64,128]{2,1,0:T(8,128)(2,1)} %lower_pivot.1, bf16[128,128]{1,0:T(8,128)(2,1)} %lower_update.1, bf16[128,256]{1,0:T(8,128)(2,1)} %parent_lower.1, ...), custom_call_target="tpu_custom_call" | custom-call | tf_op jit(solution)/shard_map/pallas_call | solution.py:525
  95.3 0.0 copy-start
  95.3 1.5 %copy.14 = f32[128,128]{1,0:T(8,128)} copy(f32[128,128]{1,0:T(8,128)} %get-tuple-element.4) | data formatting | bytes 131072
  96.8 0.0 copy-done
  96.8 0.6 copy.15
Async XLA Ops:
  95.3 1.5 %copy-start = (f32[2,64,128]{2,1,0:T(8,128)S(1)}, f32[2,64,128]{2,1,0:T(8,128)}, u32[]{:S(2)}) copy-start(f32[2,64,128]{2,1,0:T(8,128)} %get-tuple-element.5) | copy-start | bytes 196612

commit v2 on v1

v2 whole, which is shorter than its diff:
```python
import functools

import jax
import jax.numpy as jnp
from jax import lax
from jax.experimental import pallas as pl
from jax.experimental.pallas import tpu as pltpu
from jax.sharding import PartitionSpec as P

BF = jnp.bfloat16
F32 = jnp.float32
MESH = pl.DeviceIdType.MESH

Z = 8
DIST = (0, -1, 1, -2, 2, -3, 3, 4)
N_GATHER, N_SPREAD = 5, 5
SENDS = 40


def dot(left, right):
    return jnp.dot(left, right, preferred_element_type=F32)


def kernel(
    pivot_rhs,
    update_rhs,
    parent_rhs,
    lower_pivot,
    lower_update,
    parent_lower,
    parent_upper,
    upper_pivot,
    upper_update,
    maps,
    parent_out,
    child_out,
    x_pin,
    x_half,
    x_sol,
    x_sum,
    x_mid,
    a_low,
    a_par,
    a_piv,
    a_up,
    cross,
    u_half,
    moved,
    given,
    pick,
    acc,
    direct,
    g_send,
    g_recv,
    s_send,
    s_recv,
    e_send,
    e_recv,
    h_send,
    h_recv,
):
    me_p, me_r = lax.axis_index("panel"), lax.axis_index("rhs")
    core = lax.rem(me_p, 2)
    c = me_p // 2
    z, y_lo = lax.rem(c, Z), c // Z
    x, y_hi = me_r // 4, lax.rem(me_r, 4)
    mate_y = 1 - y_lo
    mate_c = mate_y * Z + z
    sib = me_p + 1 - 2 * core

    def chip(y, dist):
        return y * Z + lax.rem(z + dist + Z, Z)

    def at_z(dist):
        return chip(y_lo, dist) * 2 + core

    def at_xy(dx, dy):
        return lax.rem(x + dx + 4, 4) * 4 + lax.rem(y_hi + dy + 4, 4)

    across = mate_c * 2 + core
    goal = lax.rem(me_p, 2 * Z) * 2

    barrier = pltpu.get_barrier_semaphore()
    friends = [(at_z(d), me_r) for d in (-1, 1, -2, 2)] + [(across, me_r), (sib, me_r)]
    friends += [(me_p, at_xy(*d)) for d in ((0, -1), (0, 1), (-1, 0), (1, 0))]
    for friend in friends:
        pl.semaphore_signal(barrier, inc=1, device_id=friend, device_id_type=MESH)
    for child in range(2):
        source = c + 2 * Z * child

        @pl.when(source != me_p)
        def _():
            pl.semaphore_signal(barrier, inc=1, device_id=(source, me_r), device_id_type=MESH)

    pending = []

    def rcopy(src, dst, send, recv, device):
        return pltpu.make_async_remote_copy(
            src_ref=src, dst_ref=dst, send_sem=send, recv_sem=recv, device_id=device, device_id_type=MESH
        )

    def send(src, dst, ssem, rsem, device, when=None):
        def go():
            rcopy(src, dst, ssem, rsem, device).start()

        def done():
            rcopy(src, dst, ssem, rsem, device).wait_send()

        pending.append((when, done))
        if when is None:
            go()
        else:
            pl.when(when)(go)

    def landed(ref, sem):
        pltpu.make_async_copy(ref, ref, sem).wait()

    class Gather:
        def __init__(self, g, place, kind, cross=None):
            self.g, self.place, self.kind, self.cross, self.n = g, place, kind, cross, 0

        def sem(self, side, col, dist):
            return g_recv.at[self.g, side * 16 + col * 8 + DIST.index(dist)]

        def block(self, col, dist, side=0):
            y = y_lo if col == 0 else mate_y
            return self.place(chip(y, dist), core if side == 0 else 1 - core)

        def put(self, col, dist, to, side, col_there, dist_there, when=None, src=None):
            ref = self.block(col, dist)
            send(
                ref if src is None else src,
                ref,
                g_send.at[self.g, self.n],
                self.sem(side, col_there, dist_there),
                (to, me_r),
                when,
            )
            self.n += 1

        def along(self, col, when=None):
            for d in (2, -2, 1, -1):
                self.put(col, 0, at_z(d), 0, col, -d, when)

        def relay(self, col, d, up, down, when=None):
            if d == -2:
                self.put(col, d, at_z(1), 0, col, -3, when)
                self.put(col, d, at_z(2), 0, col, 4, up)
            if d == 2:
                self.put(col, d, at_z(-1), 0, col, 3, when)
                self.put(col, d, at_z(-2), 0, col, 4, down)

        def start(self):
            if self.kind == "first":
                self.put(0, 0, across, 0, 1, 0, src=self.cross)
            self.along(0)
            if self.kind == "full":
                self.put(0, 0, across, 0, 1, 0)
            self.put(0, 0, sib, 1, 0, 0)

        def hop(self, d):
            landed(self.block(0, d), self.sem(0, 0, d))
            self.relay(0, d, core == 0, core == 1)
            if self.kind == "full":
                self.put(0, d, across, 0, 1, d, core == 0)
            self.put(0, d, sib, 1, 0, d)

        def over(self, d):
            landed(self.block(1, d), self.sem(0, 1, d))
            if self.kind == "first":
                if d == 0:
                    self.along(1)
                self.relay(1, d, core == 0, core == 1)
            else:
                late = core == 1
                even = lax.rem(z, 2) == 0
                if d == 0:
                    self.along(1, late)
                self.relay(
                    1, d, jnp.logical_and(late, even), jnp.logical_and(late, jnp.logical_not(even)), late
                )
            self.put(1, d, sib, 1, 1, d)

        def arrive(self, col, d):
            landed(self.block(col, d, 1), self.sem(1, col, d))

        def near(self):
            if self.kind != "line":
                self.over(0)
            for d in (-2, 2, -1, 1):
                self.hop(d)

        def far(self):
            for d in (-3, 3, 4):
                self.hop(d)
            if self.kind != "line":
                for d in (-2, 2, -1, 1, -3, 3, 4):
                    self.over(d)

        def all_in(self):
            for col in range(1 if self.kind == "line" else 2):
                for d in DIST:
                    self.arrive(col, d)

    class Spread:
        def __init__(self, a, place):
            self.a, self.place, self.n = a, place, 0

        def sem(self, hop, piece):
            return s_recv.at[self.a, hop * 4 + piece]

        def block(self, hop, piece):
            dx = {0: 0, 1: -1, 2: 1, 3: 2}[hop]
            dy = {0: 0, 1: -1, 2: 1, 3: 2}[piece]
            return self.place(at_xy(dx, dy))

        def put(self, hop, piece, to, hop_there, piece_there, when=None):
            ref = self.block(hop, piece)
            send(
                ref,
                ref,
                s_send.at[self.a, self.n],
                self.sem(hop_there, piece_there),
                (me_p, to),
                when,
            )
            self.n += 1

        def start(self):
            self.put(0, 0, at_xy(0, 1), 0, 1)
            self.put(0, 0, at_xy(0, -1), 0, 2)

        def wait(self, hop, piece):
            landed(self.block(hop, piece), self.sem(hop, piece))

        def turn(self):
            self.wait(0, 1)
            self.put(0, 1, at_xy(0, 1), 0, 3, core == 0)
            self.wait(0, 2)
            self.put(0, 2, at_xy(0, -1), 0, 3, core == 1)

        def out(self, piece):
            if piece == 3:
                self.wait(0, 3)
            self.put(0, piece, at_xy(1, 0), 1, piece)
            self.put(0, piece, at_xy(-1, 0), 2, piece)

        def on(self, piece):
            self.wait(1, piece)
            self.put(1, piece, at_xy(1, 0), 3, piece, core == 0)
            self.wait(2, piece)
            self.put(2, piece, at_xy(-1, 0), 3, piece, core == 1)

        def end(self):
            for piece in range(4):
                self.wait(3, piece)

    class Extra:
        def __init__(self, e, ref, c):
            self.e, self.ref = e, ref
            self.dx = lax.rem(x - c // 4 + 4, 4)
            self.dy = lax.rem(y_hi - lax.rem(c, 4) + 4, 4)
            self.n = 0

        def put(self, to, when):
            send(self.ref, self.ref, e_send.at[self.e, self.n], e_recv.at[self.e], (me_p, to), when)
            self.n += 1

        def wait(self, when):
            @pl.when(when)
            def _():
                landed(self.ref, e_recv.at[self.e])

        def both(self, *conditions):
            return functools.reduce(jnp.logical_and, conditions)

        def start(self):
            source = self.both(self.dx == 0, self.dy == 0)
            self.put(at_xy(0, 1), source)
            self.put(at_xy(0, -1), source)
            self.put(at_xy(1, 0), source)
            self.put(at_xy(-1, 0), source)

        def turn(self):
            low, high = self.both(self.dx == 0, self.dy == 1), self.both(self.dx == 0, self.dy == 3)
            near = self.both(self.dx == 0, lax.rem(self.dy, 2) == 1)
            self.wait(near)
            self.put(at_xy(0, 1), self.both(low, core == 0))
            self.put(at_xy(0, -1), self.both(high, core == 1))
            self.put(at_xy(1, 0), near)
            self.put(at_xy(-1, 0), near)

        def out(self):
            far = self.both(self.dx == 0, self.dy == 2)
            self.wait(far)
            self.put(at_xy(1, 0), far)
            self.put(at_xy(-1, 0), far)

        def on(self):
            self.wait(lax.rem(self.dx, 2) == 1)
            self.put(at_xy(1, 0), self.both(self.dx == 1, core == 0))
            self.put(at_xy(-1, 0), self.both(self.dx == 3, core == 1))

        def end(self):
            self.wait(self.dx == 2)

    def slot(r, c=c):
        return r + (r + 15 - c) // 16

    owner = [z, Z + z]

    g_pin = Gather(0, lambda chip_at, core_at: x_pin.at[chip_at, core_at], "first", cross)
    g_sum = Gather(1, lambda chip_at, core_at: x_sum.at[chip_at, core_at], "full")
    g_mid = Gather(2, lambda chip_at, core_at: x_mid.at[chip_at, core_at], "full")
    g_sol = Gather(3, lambda chip_at, core_at: x_sol.at[:, chip_at, core_at], "full")
    g_half = Gather(4, lambda chip_at, core_at: x_half.at[:, lax.rem(chip_at, Z), core_at], "line")
    f_low = Spread(0, lambda r: a_low.at[r])
    f_par = Spread(1, lambda r: a_par.at[slot(r)])
    f_piv = [Spread(2 + j, lambda r, j=j: a_piv.at[j, slot(r, owner[j])]) for j in range(2)]
    f_up = Spread(4, lambda r: a_up.at[r])
    e_par = Extra(0, a_par.at[c + 1], c)
    e_piv = [Extra(1 + j, a_piv.at[j, owner[j] + 1], owner[j]) for j in range(2)]

    x_pin[c, core] = pivot_rhs[y_lo].astype(BF)
    cross[...] = pivot_rhs[mate_y].astype(BF)
    a_low[me_r] = lower_update[...]
    alone = (31 - me_p) // 31 + me_p // 31
    pl.semaphore_wait(barrier, len(friends) + 2 - alone)

    f_low.start()
    g_pin.start()
    f_low.out(0)

    is_low, is_high = me_r <= c, me_r >= c

    @pl.when(is_low)
    def _():
        a_par[me_r] = parent_lower[...]
        a_piv[y_lo, me_r] = lower_pivot[y_lo]

    @pl.when(is_high)
    def _():
        a_par[me_r + 1] = parent_upper[...]
        a_piv[y_lo, me_r + 1] = upper_pivot[y_lo]

    a_up[me_r] = upper_update[...]
    send(
        lower_pivot.at[mate_y],
        a_piv.at[y_lo, me_r],
        h_send.at[1, 0],
        h_recv.at[1, 0],
        (across, me_r),
        is_low,
    )
    send(
        upper_pivot.at[mate_y],
        a_piv.at[y_lo, me_r + 1],
        h_send.at[1, 1],
        h_recv.at[1, 1],
        (across, me_r),
        is_high,
    )

    start = pl.multiple_of(c * 128, 128)
    lanes = [maps[:, pl.ds(k * 2048 + start, 128)] - me_p * 128 for k in range(2)]
    low = jnp.concatenate([lanes[0][:, :64], lanes[1][:, :64]], axis=1)
    high = jnp.concatenate([lanes[0][:, 64:], lanes[1][:, 64:]], axis=1)
    targets = jnp.where(core == 0, low, high)
    rows = lax.broadcasted_iota(jnp.int32, (128, 128), 0)
    chosen = (rows == targets).astype(F32)
    pick[0] = chosen.astype(BF)
    pick[1] = chosen.T.astype(BF)

    g_pin.near()
    f_low.turn()
    f_low.out(1)
    f_low.out(2)
    g_pin.far()
    f_low.out(3)
    f_par.start()
    f_low.on(0)
    f_low.on(1)
    f_low.on(2)
    f_par.out(0)
    g_pin.all_in()
    f_low.on(3)
    f_low.end()

    def square(buffer, r):
        return buffer[r].reshape(128, 128)

    value = update_rhs[...]
    for r in range(16):
        value += dot(a_low[r], square(x_pin, r))
    u_half[...] = value.astype(BF)
    for side in range(2):
        there = goal + side
        piece = u_half.at[pl.ds(side * 64, 64)]
        land = moved.at[y_lo]
        send(piece, land, h_send.at[0, side], h_recv.at[0, y_lo], (there, me_r), there != me_p)

        @pl.when(there == me_p)
        def _():
            pltpu.make_async_copy(piece, land, h_recv.at[0, y_lo]).start()

    f_par.turn()
    f_par.out(1)
    f_par.out(2)
    e_par.start()

    @pl.when(me_r <= mate_c)
    def _():
        ref = a_piv.at[mate_y, me_r]
        landed(ref, h_recv.at[1, 0])

    @pl.when(me_r >= mate_c)
    def _():
        ref = a_piv.at[mate_y, me_r + 1]
        landed(ref, h_recv.at[1, 1])

    for child in range(2):
        landed(moved.at[child], h_recv.at[0, child])
    total = parent_rhs[...] + dot(pick[0], moved[...].reshape(128, 128))
    x_sum[c, core] = total.astype(BF)
    g_sum.start()

    g_sum.near()
    f_par.out(3)
    f_par.on(0)
    f_par.on(1)
    f_par.on(2)
    for j in range(2):
        f_piv[j].start()
        f_piv[j].out(0)
    g_sum.far()
    e_par.turn()
    f_par.on(3)
    g_sum.all_in()
    f_par.end()

    def pair(buffer, r):
        return buffer[r].reshape(256, 128)

    acc[...] = jnp.zeros_like(acc)
    for r in range(16):

        @pl.when(r <= c)
        def _():
            acc[...] += dot(a_par[r], pair(x_sum, r))

    x_mid[c, core] = acc[...].astype(BF)
    g_mid.start()

    for j in range(2):
        f_piv[j].turn()
        f_piv[j].out(1)
        f_piv[j].out(2)
        e_piv[j].start()
    g_mid.near()
    e_par.out()
    for j in range(2):
        f_piv[j].out(3)
        for piece in range(3):
            f_piv[j].on(piece)
    f_up.start()
    f_up.out(0)
    g_mid.far()
    for j in range(2):
        f_piv[j].on(3)
        e_piv[j].turn()
    e_par.on()
    f_up.turn()
    f_up.out(1)
    f_up.out(2)
    g_mid.all_in()
    e_par.end()

    acc[...] = jnp.zeros_like(acc)
    for r in range(16):

        @pl.when(r >= c)
        def _():
            acc[...] += dot(a_par[r + 1], pair(x_mid, r))

    picked = dot(pick[1], acc[...].astype(BF)).astype(BF)
    x_sol[:, c, core] = picked.reshape(2, 64, 128)
    g_sol.start()
    parent_out[...] = acc[...]

    for j in range(2):
        f_piv[j].end()
        e_piv[j].out()
    f_up.out(3)
    direct[...] = jnp.zeros_like(direct)
    for r in range(16):
        for j in range(2):

            @pl.when(r <= owner[j])
            def _():
                direct[j] += dot(a_piv[j, r], square(x_pin, r))

    x_half[:, z, core] = direct[...].astype(BF)
    g_half.start()
    g_sol.near()
    for piece in range(3):
        f_up.on(piece)
    g_half.near()
    g_sol.far()
    for j in range(2):
        e_piv[j].on()
    g_half.far()
    f_up.on(3)
    g_half.all_in()
    for j in range(2):
        e_piv[j].end()

    direct[...] = jnp.zeros_like(direct)
    for r in range(16):
        for j in range(2):

            @pl.when(r >= owner[j])
            def _():
                direct[j] += dot(a_piv[j, r + 1], x_half[r // 8, r % 8].reshape(128, 128))

    send(
        direct.at[mate_y],
        given,
        h_send.at[2, 0],
        h_recv.at[2, 0],
        (across, me_r),
    )
    g_sol.all_in()
    f_up.end()
    for k in range(2):
        value = dot(a_up[0, k], square(x_sol.at[k], 0))
        for r in range(1, 16):
            value += dot(a_up[r, k], square(x_sol.at[k], r))
        child_out[k] = value
    child_out[y_lo] += direct[y_lo]
    landed(given, h_recv.at[2, 0])
    child_out[mate_y] += given[...]

    for when, done in pending:
        if when is None:
            done()
        else:
            pl.when(when)(done)


def shards(*arguments):
    *arrays, maps = arguments
    vm = pltpu.VMEM
    dma = pltpu.SemaphoreType.DMA
    return pl.pallas_call(
        kernel,
        out_shape=(
            jax.ShapeDtypeStruct((128, 128), F32),
            jax.ShapeDtypeStruct((2, 64, 128), F32),
        ),
        in_specs=[pl.BlockSpec(memory_space=pltpu.VMEM)] * 10,
        out_specs=(pl.BlockSpec(memory_space=pltpu.VMEM),) * 2,
        scratch_shapes=[
            vm((16, 2, 64, 128), BF),
            vm((2, Z, 2, 64, 128), BF),
            vm((2, 16, 2, 64, 128), BF),
            vm((16, 2, 128, 128), BF),
            vm((16, 2, 128, 128), BF),
            vm((16, 128, 128), BF),
            vm((17, 128, 256), BF),
            vm((2, 17, 64, 128), BF),
            vm((16, 2, 64, 128), BF),
            vm((64, 128), BF),
            vm((128, 128), BF),
            vm((2, 64, 128), BF),
            vm((64, 128), F32),
            vm((2, 128, 128), BF),
            vm((128, 128), F32),
            vm((2, 64, 128), F32),
            dma((N_GATHER, SENDS)),
            dma((N_GATHER, 32)),
            dma((N_SPREAD, 20)),
            dma((N_SPREAD, 16)),
            dma((3, 12)),
            dma((3,)),
            dma((3, 2)),
            dma((3, 2)),
        ],
        compiler_params=pltpu.CompilerParams(
            collective_id=0, has_side_effects=True, vmem_limit_bytes=60 * 1024 * 1024
        ),
    )(*arrays, maps.reshape(1, -1))


def solution(mesh):
    placed = (
        P(None, "panel", "rhs"),
        P("panel", "rhs"),
        P("panel", "rhs"),
        P(None, "panel", "rhs"),
        P("panel", "rhs"),
        P("panel", "rhs"),
        P("panel", "rhs"),
        P(None, "panel", "rhs"),
        P(None, "panel", "rhs"),
        P(),
    )
    return jax.shard_map(
        shards,
        mesh=mesh,
        in_specs=placed,
        out_specs=(P("panel", "rhs"), P(None, "panel", "rhs")),
        check_vma=False,
    )
```

time: 97.6 us -> 101 us (1.035)
  the two profiles are of different devices: /device:TPU:1 before, /device:TPU:16 now
where the time goes in v2:
time: 101 us
  Pallas kernels  98.2 us (97%)
  local copies, waits for them, and re-layouts  2.14 us (2%)
    pallas_call x1, Pallas kernels, shards(): pl.pallas_call(kernel, out_shape=(jax.ShapeDtypeStruct((128, 128), F32),...  98.2 us
    unnamed x4, local copies, waits for them, and re-layouts  2.14 us

profile of v2, /device:TPU:16, one launch (start us, length us, event | category | flops | bytes accessed | tf_op | source)
XLA Modules:
  0.0 101.0 jit_solution(4576535746748864477)
XLA Ops:
  0.6 98.2 %shard_map.113 = (f32[128,128]{1,0:T(8,128)}, f32[2,64,128]{2,1,0:T(8,128)}) custom-call(f32[2,64,128]{2,1,0:T(8,128)} %pivot_rhs.1, f32[128,128]{1,0:T(8,128)} %update_rhs.1, f32[128,128]{1,0:T(8,128)} %parent_rhs.1, bf16[2,64,128]{2,1,0:T(8,128)(2,1)} %lower_pivot.1, bf16[128,128]{1,0:T(8,128)(2,1)} %lower_update.1, bf16[128,256]{1,0:T(8,128)(2,1)} %parent_lower.1, ...), custom_call_target="tpu_custom_call" | custom-call | tf_op jit(solution)/shard_map/pallas_call | solution.py:554
  98.8 0.0 copy-start
  98.8 1.5 %copy.14 = f32[128,128]{1,0:T(8,128)} copy(f32[128,128]{1,0:T(8,128)} %get-tuple-element.4) | data formatting | bytes 131072
  100.3 0.0 copy-done
  100.3 0.6 copy.15
Async XLA Ops:
  98.8 1.5 %copy-start = (f32[2,64,128]{2,1,0:T(8,128)S(1)}, f32[2,64,128]{2,1,0:T(8,128)}, u32[]{:S(2)}) copy-start(f32[2,64,128]{2,1,0:T(8,128)} %get-tuple-element.5) | copy-start | bytes 196612

commit v3 on v2

v3 whole, which is shorter than its diff:
```python
import functools

import jax
import jax.numpy as jnp
from jax import lax
from jax.experimental import pallas as pl
from jax.experimental.pallas import tpu as pltpu
from jax.sharding import PartitionSpec as P

BF = jnp.bfloat16
F32 = jnp.float32
MESH = pl.DeviceIdType.MESH

Z = 8
DIST = (0, -1, 1, -2, 2, -3, 3, 4)
HOP = {-2: 0, 2: 1, -1: 2, 1: 2, -3: 3, 3: 3, 4: 4}
OVER = {0: 5, -2: 6, 2: 7, -1: 8, 1: 8, -3: 9, 3: 9, 4: 10}
SIBLING = 11
N_GATHER, N_SPREAD, N_EXTRA, N_SEND = 5, 5, 3, 64
RULER = 96


def dot(left, right):
    return jnp.dot(left, right, preferred_element_type=F32)


def kernel(
    pivot_rhs,
    update_rhs,
    parent_rhs,
    lower_pivot,
    lower_update,
    parent_lower,
    parent_upper,
    upper_pivot,
    upper_update,
    maps,
    parent_out,
    child_out,
    x_pin,
    x_half,
    x_sel,
    x_sum,
    x_mid,
    a_low,
    a_par,
    a_piv,
    a_up,
    a_back,
    cross,
    u_half,
    moved,
    given,
    pick,
    direct,
    ruler,
    send_sem,
    g_recv,
    s_recv,
    e_recv,
    h_recv,
):
    me_p, me_r = lax.axis_index("panel"), lax.axis_index("rhs")
    core = lax.rem(me_p, 2)
    c = me_p // 2
    z, y_lo = lax.rem(c, Z), c // Z
    x, y_hi = me_r // 4, lax.rem(me_r, 4)
    mate_y = 1 - y_lo
    mate_c = mate_y * Z + z
    sib = me_p + 1 - 2 * core

    def chip(y, dist):
        return y * Z + lax.rem(z + dist + Z, Z)

    def at_z(dist):
        return chip(y_lo, dist) * 2 + core

    def at_xy(dx, dy):
        return lax.rem(x + dx + 4, 4) * 4 + lax.rem(y_hi + dy + 4, 4)

    across = mate_c * 2 + core
    goal = lax.rem(me_p, 2 * Z) * 2

    barrier = pltpu.get_barrier_semaphore()
    friends = [(at_z(d), me_r) for d in (-1, 1, -2, 2)] + [(across, me_r), (sib, me_r)]
    friends += [(me_p, at_xy(*d)) for d in ((0, -1), (0, 1), (-1, 0), (1, 0))]
    for friend in friends:
        pl.semaphore_signal(barrier, inc=1, device_id=friend, device_id_type=MESH)
    for child in range(2):
        source = c + 2 * Z * child

        @pl.when(source != me_p)
        def _():
            pl.semaphore_signal(barrier, inc=1, device_id=(source, me_r), device_id_type=MESH)

    book = {}

    def send(src, dst, units, recv, device, group, key="all", when=None):
        entry = book.setdefault((group, key), [len(book), 0, when])
        entry[1] += units
        copy = pltpu.make_async_remote_copy(
            src_ref=src,
            dst_ref=dst,
            send_sem=send_sem.at[entry[0]],
            recv_sem=recv,
            device_id=device,
            device_id_type=MESH,
        )
        if when is None:
            copy.start()
        else:
            pl.when(when)(copy.start)

    def landed(units, sem):
        ref = ruler.at[pl.ds(0, units)]
        pltpu.make_async_copy(ref, ref, sem).wait()

    first_core, second_core = core == 0, core == 1
    even = jnp.logical_and(second_core, lax.rem(z, 2) == 0)
    odd = jnp.logical_and(second_core, lax.rem(z, 2) == 1)

    class Gather:
        def __init__(self, g, place, units, kind, cross=None):
            self.g, self.place, self.units, self.kind, self.cross = g, place, units, kind, cross

        def sem(self, side, col, dist):
            spot = SIBLING if side else OVER[dist] if col else HOP[dist]
            return g_recv.at[self.g, spot]

        def block(self, col, dist, side=0):
            y = y_lo if col == 0 else mate_y
            return self.place(chip(y, dist), core if side == 0 else 1 - core)

        def put(self, col, dist, to, side, col_there, dist_there, key="all", when=None, src=None):
            ref = self.block(col, dist)
            send(
                ref if src is None else src,
                ref,
                self.units,
                self.sem(side, col_there, dist_there),
                (to, me_r),
                ("g", self.g),
                key,
                when,
            )

        def along(self, col, key="all", when=None):
            for d in (2, -2, 1, -1):
                self.put(col, 0, at_z(d), 0, col, -d, key, when)

        def relay(self, col, d, up, down, key="all", when=None):
            if d == -2:
                self.put(col, d, at_z(1), 0, col, -3, key, when)
                self.put(col, d, at_z(2), 0, col, 4, *up)
            if d == 2:
                self.put(col, d, at_z(-1), 0, col, 3, key, when)
                self.put(col, d, at_z(-2), 0, col, 4, *down)

        def start(self):
            if self.kind == "first":
                self.put(0, 0, across, 0, 1, 0, src=self.cross)
            self.along(0)
            if self.kind == "full":
                self.put(0, 0, across, 0, 1, 0)
            self.put(0, 0, sib, 1, 0, 0)

        def hop(self, *dists):
            landed(self.units * len(dists), self.sem(0, 0, dists[0]))
            for d in dists:
                self.relay(0, d, ("first", first_core), ("second", second_core))
                if self.kind == "full":
                    self.put(0, d, across, 0, 1, d, "first", first_core)
                self.put(0, d, sib, 1, 0, d)

        def over(self, *dists):
            landed(self.units * len(dists), self.sem(0, 1, dists[0]))
            for d in dists:
                if self.kind == "first":
                    if d == 0:
                        self.along(1)
                    self.relay(1, d, ("first", first_core), ("second", second_core))
                else:
                    if d == 0:
                        self.along(1, "second", second_core)
                    self.relay(1, d, ("even", even), ("odd", odd), "second", second_core)
                self.put(1, d, sib, 1, 1, d)

        def near(self):
            if self.kind != "line":
                self.over(0)
            self.hop(-2)
            self.hop(2)
            self.hop(-1, 1)

        def far(self):
            self.hop(-3, 3)
            self.hop(4)

        def near_over(self):
            self.over(-2)
            self.over(2)
            self.over(-1, 1)

        def far_over(self):
            self.over(-3, 3)
            self.over(4)

        def all_in(self):
            landed(self.units * (8 if self.kind == "line" else 16), self.sem(1, 0, 0))

    class Spread:
        def __init__(self, a, places, units):
            self.a, self.places, self.units = a, places, units

        def sem(self, hop, piece):
            spot = {0: piece - 1, 1: 3 + piece // 3, 2: 5 + piece // 3, 3: 7}[hop]
            return s_recv.at[self.a, spot]

        def put(self, hop, piece, to, hop_there, piece_there, key="all", when=None):
            dx = {0: 0, 1: -1, 2: 1, 3: 2}[hop]
            dy = {0: 0, 1: -1, 2: 1, 3: 2}[piece]
            for place in self.places:
                ref = place(at_xy(dx, dy))
                send(
                    ref,
                    ref,
                    self.units,
                    self.sem(hop_there, piece_there),
                    (me_p, to),
                    ("s", self.a),
                    key,
                    when,
                )

        def start(self):
            self.put(0, 0, at_xy(0, 1), 0, 1)
            self.put(0, 0, at_xy(0, -1), 0, 2)

        def wait(self, hop, piece, count=1):
            landed(self.units * len(self.places) * count, self.sem(hop, piece))

        def turn(self):
            self.wait(0, 1)
            self.put(0, 1, at_xy(0, 1), 0, 3, "first", first_core)
            self.wait(0, 2)
            self.put(0, 2, at_xy(0, -1), 0, 3, "second", second_core)

        def out(self, *pieces):
            for piece in pieces:
                if piece == 3:
                    self.wait(0, 3)
                self.put(0, piece, at_xy(1, 0), 1, piece)
                self.put(0, piece, at_xy(-1, 0), 2, piece)

        def on(self):
            self.wait(1, 0, 3)
            for piece in range(3):
                self.put(1, piece, at_xy(1, 0), 3, piece, "first", first_core)
            self.wait(2, 0, 3)
            for piece in range(3):
                self.put(2, piece, at_xy(-1, 0), 3, piece, "second", second_core)

        def on_last(self):
            self.wait(1, 3)
            self.put(1, 3, at_xy(1, 0), 3, 3, "first", first_core)
            self.wait(2, 3)
            self.put(2, 3, at_xy(-1, 0), 3, 3, "second", second_core)

        def end(self):
            self.wait(3, 0, 4)

    class Extra:
        def __init__(self, e, ref, units, c):
            self.e, self.ref, self.units = e, ref, units
            self.dx = lax.rem(x - c // 4 + 4, 4)
            self.dy = lax.rem(y_hi - lax.rem(c, 4) + 4, 4)

        def put(self, to, key, when):
            send(self.ref, self.ref, self.units, e_recv.at[self.e], (me_p, to), ("e", self.e), key, when)

        def wait(self, when):
            @pl.when(when)
            def _():
                landed(self.units, e_recv.at[self.e])

        def both(self, *conditions):
            return functools.reduce(jnp.logical_and, conditions)

        def start(self):
            source = self.both(self.dx == 0, self.dy == 0)
            for to in ((0, 1), (0, -1), (1, 0), (-1, 0)):
                self.put(at_xy(*to), "source", source)

        def turn(self):
            low, high = self.both(self.dx == 0, self.dy == 1), self.both(self.dx == 0, self.dy == 3)
            near = self.both(self.dx == 0, lax.rem(self.dy, 2) == 1)
            self.wait(near)
            self.put(at_xy(0, 1), "low", self.both(low, first_core))
            self.put(at_xy(0, -1), "high", self.both(high, second_core))
            self.put(at_xy(1, 0), "near", near)
            self.put(at_xy(-1, 0), "near", near)

        def out(self):
            far = self.both(self.dx == 0, self.dy == 2)
            self.wait(far)
            self.put(at_xy(1, 0), "far", far)
            self.put(at_xy(-1, 0), "far", far)

        def on(self):
            self.wait(lax.rem(self.dx, 2) == 1)
            self.put(at_xy(1, 0), "left", self.both(self.dx == 1, first_core))
            self.put(at_xy(-1, 0), "right", self.both(self.dx == 3, second_core))

        def end(self):
            self.wait(self.dx == 2)

    def slot(r, c=c):
        return r + (r + 15 - c) // 16 * 16

    owner = [z, Z + z]

    g_pin = Gather(0, lambda chip_at, core_at: x_pin.at[chip_at, core_at], 1, "first", cross)
    g_sum = Gather(1, lambda chip_at, core_at: x_sum.at[chip_at, core_at], 2, "full")
    g_mid = Gather(2, lambda chip_at, core_at: x_mid.at[chip_at, core_at], 2, "full")
    g_sel = Gather(3, lambda chip_at, core_at: x_sel.at[chip_at, :, core_at], 4, "full")
    g_half = Gather(4, lambda chip_at, core_at: x_half.at[lax.rem(chip_at, Z), core_at], 2, "line")
    f_low = Spread(0, [lambda r: a_low.at[r]], 2)
    f_par = Spread(1, [lambda r: a_par.at[slot(r)]], 4)
    f_piv = Spread(2, [lambda r, j=j: a_piv.at[slot(r, owner[j]), j] for j in range(2)], 1)
    f_up = Spread(3, [lambda r: a_up.at[r]], 2)
    f_back = Spread(4, [lambda r: a_back.at[r]], 4)
    e_par = Extra(0, a_par.at[16 + c], 4, c)
    e_piv = [Extra(1 + j, a_piv.at[16 + owner[j], j], 1, owner[j]) for j in range(2)]
    extras = [e_par] + e_piv

    x_pin[c, core] = pivot_rhs[y_lo].astype(BF)
    cross[...] = pivot_rhs[mate_y].astype(BF)
    a_low[me_r] = lower_update[...]
    alone = (31 - me_p) // 31 + me_p // 31
    pl.semaphore_wait(barrier, len(friends) + 2 - alone)

    f_low.start()
    g_pin.start()
    f_low.out(0)

    is_low, is_high = me_r <= c, me_r >= c
    a_up[me_r] = upper_update[...]
    f_up.start()
    f_up.out(0)

    @pl.when(is_low)
    def _():
        a_par[me_r] = parent_lower[...]
        a_piv[me_r, y_lo] = lower_pivot[y_lo]

    @pl.when(is_high)
    def _():
        a_par[16 + me_r] = parent_upper[...]
        a_piv[16 + me_r, y_lo] = upper_pivot[y_lo]

    @pl.loop(0, 16)
    def _(r):
        @pl.when(r > c)
        def _():
            a_par[r] = jnp.zeros((128, 256), BF)

        @pl.when(r < c)
        def _():
            a_par[16 + r] = jnp.zeros((128, 256), BF)

        for j in range(2):

            @pl.when(r > owner[j])
            def _():
                a_piv[r, j] = jnp.zeros((64, 128), BF)

            @pl.when(r < owner[j])
            def _():
                a_piv[16 + r, j] = jnp.zeros((64, 128), BF)

    def swap(src, dst, spot, when):
        send(src, dst, 1, h_recv.at[spot], (across, me_r), ("swap", spot), "on", when)

    swap(lower_pivot.at[mate_y], a_piv.at[me_r, y_lo], 2, is_low)
    swap(upper_pivot.at[mate_y], a_piv.at[16 + me_r, y_lo], 3, is_high)

    start = pl.multiple_of(c * 128, 128)
    lanes = [maps[:, pl.ds(k * 2048 + start, 128)] - me_p * 128 for k in range(2)]
    low = jnp.concatenate([lanes[0][:, :64], lanes[1][:, :64]], axis=1)
    high = jnp.concatenate([lanes[0][:, 64:], lanes[1][:, 64:]], axis=1)
    targets = jnp.where(core == 0, low, high)
    rows = lax.broadcasted_iota(jnp.int32, (128, 128), 0)
    chosen = (rows == targets).astype(F32)
    pick[...] = chosen.astype(BF)
    x_sel[c, :, core] = dot(chosen.T.astype(BF), parent_upper[...]).astype(BF).reshape(2, 64, 256)

    g_pin.near()
    f_low.turn()
    f_low.out(1, 2)
    g_pin.far()
    g_pin.near_over()
    f_low.out(3)
    f_low.on()
    f_up.turn()
    f_up.out(1, 2)
    g_sel.start()
    g_pin.far_over()
    f_low.on_last()
    g_pin.all_in()
    f_low.end()

    def square(buffer, r):
        return buffer[r].reshape(128, 128)

    def pair(buffer, r):
        return buffer[r].reshape(256, 128)

    def gemm(value, left, right):
        for r in range(16):
            value += dot(left(r), right(r))
        return value

    value = gemm(update_rhs[...], lambda r: a_low[r], lambda r: square(x_pin, r))
    u_half[...] = value.astype(BF)
    for side in range(2):
        there = goal + side
        piece = u_half.at[pl.ds(side * 64, 64)]
        land = moved.at[y_lo]
        send(piece, land, 1, h_recv.at[y_lo], (there, me_r), ("move", side), "on", there != me_p)

        @pl.when(there == me_p)
        def _():
            pltpu.make_async_copy(piece, land, h_recv.at[y_lo]).start()

    g_sel.near()
    f_up.out(3)

    @pl.when(me_r <= mate_c)
    def _():
        landed(1, h_recv.at[2])

    @pl.when(me_r >= mate_c)
    def _():
        landed(1, h_recv.at[3])

    f_piv.start()
    f_piv.out(0)
    f_par.start()
    f_par.out(0)
    for k in range(2):
        landed(1, h_recv.at[k])

    total = parent_rhs[...] + dot(pick[...], moved[...].reshape(128, 128))
    x_sum[c, core] = total.astype(BF)
    g_sum.start()
    g_sel.far()
    f_up.on()
    f_piv.turn()
    f_piv.out(1, 2)
    g_sum.near()
    f_par.turn()
    f_par.out(1, 2)
    f_piv.out(3)
    f_up.on_last()
    g_sel.near_over()
    g_sum.far()
    f_par.out(3)
    f_piv.on()
    g_sel.far_over()
    for extra in extras:
        extra.start()
    g_sum.near_over()
    f_piv.on_last()
    f_par.on()

    g_sel.all_in()
    f_up.end()
    for k in range(2):
        value = gemm(
            jnp.zeros((64, 256), F32), lambda r: a_up[r, k], lambda r: x_sel[r, k].reshape(128, 256)
        )
        a_back[me_r, k * 64 : k * 64 + 64] = value.astype(BF)
    f_back.start()
    f_back.out(0)
    g_sum.far_over()
    f_par.on_last()
    f_piv.end()
    g_sum.all_in()
    f_par.end()

    value = gemm(jnp.zeros((128, 128), F32), lambda r: a_par[r], lambda r: pair(x_sum, r))
    x_mid[c, core] = value.astype(BF)
    g_mid.start()

    value = gemm(jnp.zeros((128, 128), F32), lambda r: square(a_piv, r), lambda r: square(x_pin, r))
    x_half[z, core] = value.astype(BF).reshape(2, 64, 128)
    g_half.start()
    for extra in extras:
        extra.turn()
    f_back.turn()
    f_back.out(1, 2)
    g_mid.near()
    g_half.near()
    for extra in extras:
        extra.out()
    f_back.out(3)
    g_mid.far()
    g_half.far()
    f_back.on()
    for extra in extras:
        extra.on()
    g_mid.near_over()
    for extra in extras:
        extra.end()
    g_half.all_in()

    def half_rows(r):
        return jnp.concatenate([x_half[r % Z, i, r // Z] for i in range(2)], axis=0)

    value = gemm(jnp.zeros((128, 128), F32), lambda r: square(a_piv, 16 + r), half_rows)
    direct[...] = value.reshape(2, 64, 128)
    send(direct.at[mate_y], given, 2, h_recv.at[4], (across, me_r), ("swap", 4))
    f_back.on_last()
    g_mid.far_over()
    f_back.end()
    landed(2, h_recv.at[4])
    g_mid.all_in()

    parent_out[...] = gemm(jnp.zeros((128, 128), F32), lambda r: a_par[16 + r], lambda r: pair(x_mid, r))
    value = gemm(jnp.zeros((128, 128), F32), lambda r: a_back[r], lambda r: pair(x_mid, r))
    child_out[...] = value.reshape(2, 64, 128)
    child_out[y_lo] += direct[y_lo]
    child_out[mate_y] += given[...]

    for spot, units, when in book.values():

        def done():
            landed(units, send_sem.at[spot])

        if when is None:
            done()
        else:
            pl.when(when)(done)


def shards(*arguments):
    *arrays, maps = arguments
    vm = pltpu.VMEM
    dma = pltpu.SemaphoreType.DMA
    return pl.pallas_call(
        kernel,
        out_shape=(
            jax.ShapeDtypeStruct((128, 128), F32),
            jax.ShapeDtypeStruct((2, 64, 128), F32),
        ),
        in_specs=[pl.BlockSpec(memory_space=pltpu.VMEM)] * 10,
        out_specs=(pl.BlockSpec(memory_space=pltpu.VMEM),) * 2,
        scratch_shapes=[
            vm((16, 2, 64, 128), BF),
            vm((Z, 2, 2, 64, 128), BF),
            vm((16, 2, 2, 64, 256), BF),
            vm((16, 2, 128, 128), BF),
            vm((16, 2, 128, 128), BF),
            vm((16, 128, 128), BF),
            vm((32, 128, 256), BF),
            vm((32, 2, 64, 128), BF),
            vm((16, 2, 64, 128), BF),
            vm((16, 128, 256), BF),
            vm((64, 128), BF),
            vm((128, 128), BF),
            vm((2, 64, 128), BF),
            vm((64, 128), F32),
            vm((128, 128), BF),
            vm((2, 64, 128), F32),
            vm((RULER, 64, 128), BF),
            dma((N_SEND,)),
            dma((N_GATHER, 12)),
            dma((N_SPREAD, 8)),
            dma((N_EXTRA,)),
            dma((5,)),
        ],
        compiler_params=pltpu.CompilerParams(
            collective_id=0, has_side_effects=True, vmem_limit_bytes=60 * 1024 * 1024
        ),
    )(*arrays, maps.reshape(1, -1))


def solution(mesh):
    placed = (
        P(None, "panel", "rhs"),
        P("panel", "rhs"),
        P("panel", "rhs"),
        P(None, "panel", "rhs"),
        P("panel", "rhs"),
        P("panel", "rhs"),
        P("panel", "rhs"),
        P(None, "panel", "rhs"),
        P(None, "panel", "rhs"),
        P(),
    )
    return jax.shard_map(
        shards,
        mesh=mesh,
        in_specs=placed,
        out_specs=(P("panel", "rhs"), P(None, "panel", "rhs")),
        check_vma=False,
    )
```

time: 101 us -> 81.3 us (0.80)
  the two profiles are of different devices: /device:TPU:16 before, /device:TPU:1 now
where the time goes in v3:
time: 81.3 us; the launch traced here: 80.7 us
  Pallas kernels  77.9 us (96%)
  local copies, waits for them, and re-layouts  2.14 us (3%)
    pallas_call x1, Pallas kernels, shards(): pl.pallas_call(kernel, out_shape=(jax.ShapeDtypeStruct((128, 128), F32),...  77.9 us
    unnamed x4, local copies, waits for them, and re-layouts  2.14 us

profile of v3, /device:TPU:1, one launch (start us, length us, event | category | flops | bytes accessed | tf_op | source)
XLA Modules:
  0.0 80.7 jit_solution(4984437399776784517)
XLA Ops:
  0.6 77.9 %shard_map.113 = (f32[128,128]{1,0:T(8,128)}, f32[2,64,128]{2,1,0:T(8,128)}) custom-call(f32[2,64,128]{2,1,0:T(8,128)} %pivot_rhs.1, f32[128,128]{1,0:T(8,128)} %update_rhs.1, f32[128,128]{1,0:T(8,128)} %parent_rhs.1, bf16[2,64,128]{2,1,0:T(8,128)(2,1)} %lower_pivot.1, bf16[128,128]{1,0:T(8,128)(2,1)} %lower_update.1, bf16[128,256]{1,0:T(8,128)(2,1)} %parent_lower.1, ...), custom_call_target="tpu_custom_call" | custom-call | tf_op jit(solution)/shard_map/pallas_call | solution.py:550
  78.5 0.0 copy-start
  78.5 1.5 %copy.14 = f32[128,128]{1,0:T(8,128)} copy(f32[128,128]{1,0:T(8,128)} %get-tuple-element.4) | data formatting | bytes 131072
  80.0 0.0 copy-done
  80.0 0.6 copy.15
Async XLA Ops:
  78.5 1.5 %copy-start = (f32[2,64,128]{2,1,0:T(8,128)S(1)}, f32[2,64,128]{2,1,0:T(8,128)}, u32[]{:S(2)}) copy-start(f32[2,64,128]{2,1,0:T(8,128)} %get-tuple-element.5) | copy-start | bytes 196612

commit v4 on v3

--- a/solution.py
+++ b/solution.py
@@ -16,7 +16,7 @@
 HOP = {-2: 0, 2: 1, -1: 2, 1: 2, -3: 3, 3: 3, 4: 4}
 OVER = {0: 5, -2: 6, 2: 7, -1: 8, 1: 8, -3: 9, 3: 9, 4: 10}
 SIBLING = 11
-N_GATHER, N_SPREAD, N_EXTRA, N_SEND = 5, 5, 3, 64
+N_GATHER, N_SPREAD, N_EXTRA, N_SEND = 6, 4, 3, 56
 RULER = 96
 
 
@@ -39,21 +39,28 @@
     child_out,
     x_pin,
     x_half,
-    x_sel,
+    x_sol,
     x_sum,
+    x_rhs,
     x_mid,
     a_low,
     a_par,
     a_piv,
     a_up,
-    a_back,
     cross,
-    u_half,
-    moved,
+    a_sum,
+    acc,
     given,
     pick,
     direct,
+    pivot_in,
+    update_in,
+    parent_in,
+    lower_piv_in,
+    upper_piv_in,
+    maps_in,
     ruler,
+    load_sem,
     send_sem,
     g_recv,
     s_recv,
@@ -78,20 +85,38 @@
     def at_xy(dx, dy):
         return lax.rem(x + dx + 4, 4) * 4 + lax.rem(y_hi + dy + 4, 4)
 
+    def beside(dist):
+        return chip(mate_y, dist) * 2 + core
+
     across = mate_c * 2 + core
-    goal = lax.rem(me_p, 2 * Z) * 2
 
     barrier = pltpu.get_barrier_semaphore()
     friends = [(at_z(d), me_r) for d in (-1, 1, -2, 2)] + [(across, me_r), (sib, me_r)]
-    friends += [(me_p, at_xy(*d)) for d in ((0, -1), (0, 1), (-1, 0), (1, 0))]
+    friends += [(beside(d), me_r) for d in (-1, 1, -2, 2)]
+    friends += [(me_p, at_xy(*d)) for d in ((0, -1), (0, 1), (-1, 0), (1, 0), (0, 2), (2, 0))]
     for friend in friends:
         pl.semaphore_signal(barrier, inc=1, device_id=friend, device_id_type=MESH)
-    for child in range(2):
-        source = c + 2 * Z * child
-
-        @pl.when(source != me_p)
-        def _():
-            pl.semaphore_signal(barrier, inc=1, device_id=(source, me_r), device_id_type=MESH)
+    is_low, is_high = me_r <= c, me_r >= c
+
+    def load(src, dst, spot):
+        pltpu.make_async_copy(src, dst, load_sem.at[spot]).start()
+
+    load(lower_update, a_low.at[me_r], 0)
+    load(pivot_rhs, pivot_in, 1)
+    load(maps, maps_in, 2)
+    load(upper_update, a_up.at[me_r], 2)
+    load(lower_pivot, lower_piv_in, 2)
+    load(upper_pivot, upper_piv_in, 2)
+    load(update_rhs, update_in, 2)
+    load(parent_rhs, parent_in, 2)
+
+    @pl.when(is_low)
+    def _():
+        load(parent_lower, a_par.at[me_r], 3)
+
+    @pl.when(is_high)
+    def _():
+        load(parent_upper, a_par.at[16 + me_r], 4)
 
     book = {}
 
@@ -157,11 +182,18 @@
                 self.put(col, d, at_z(-2), 0, col, 4, *down)
 
         def start(self):
-            if self.kind == "first":
+            if self.kind == "both":
+                for d in (2, -2):
+                    self.put(0, 0, at_z(d), 0, 0, -d)
+                    self.put(0, 0, beside(d), 0, 1, -d, src=self.cross)
+                for d in (1, -1):
+                    self.put(0, 0, at_z(d), 0, 0, -d)
+                    if self.cross is not None:
+                        self.put(0, 0, beside(d), 0, 1, -d, src=self.cross)
+            else:
+                self.along(0)
+            if self.kind != "line":
                 self.put(0, 0, across, 0, 1, 0, src=self.cross)
-            self.along(0)
-            if self.kind == "full":
-                self.put(0, 0, across, 0, 1, 0)
             self.put(0, 0, sib, 1, 0, 0)
 
         def hop(self, *dists):
@@ -170,14 +202,14 @@
                 self.relay(0, d, ("first", first_core), ("second", second_core))
                 if self.kind == "full":
                     self.put(0, d, across, 0, 1, d, "first", first_core)
+                if self.kind == "both" and self.cross is None and d in (-1, 1):
+                    self.put(0, d, across, 0, 1, d)
                 self.put(0, d, sib, 1, 0, d)
 
         def over(self, *dists):
             landed(self.units * len(dists), self.sem(0, 1, dists[0]))
             for d in dists:
-                if self.kind == "first":
-                    if d == 0:
-                        self.along(1)
+                if self.kind == "both":
                     self.relay(1, d, ("first", first_core), ("second", second_core))
                 else:
                     if d == 0:
@@ -186,15 +218,28 @@
                 self.put(1, d, sib, 1, 1, d)
 
         def near(self):
-            if self.kind != "line":
+            if self.kind == "full":
                 self.over(0)
             self.hop(-2)
             self.hop(2)
+            if self.kind == "both":
+                self.over(-2)
+                self.over(2)
             self.hop(-1, 1)
+            if self.kind == "both":
+                self.over(0)
+                if self.cross is not None:
+                    self.over(-1, 1)
 
         def far(self):
+            if self.kind == "both" and self.cross is None:
+                self.over(-1, 1)
             self.hop(-3, 3)
+            if self.kind == "both":
+                self.over(-3, 3)
             self.hop(4)
+            if self.kind == "both":
+                self.over(4)
 
         def near_over(self):
             self.over(-2)
@@ -209,8 +254,8 @@
             landed(self.units * (8 if self.kind == "line" else 16), self.sem(1, 0, 0))
 
     class Spread:
-        def __init__(self, a, places, units):
-            self.a, self.places, self.units = a, places, units
+        def __init__(self, a, places, units, jump=False):
+            self.a, self.places, self.units, self.jump = a, places, units, jump
 
         def sem(self, hop, piece):
             spot = {0: piece - 1, 1: 3 + piece // 3, 2: 5 + piece // 3, 3: 7}[hop]
@@ -235,15 +280,19 @@
         def start(self):
             self.put(0, 0, at_xy(0, 1), 0, 1)
             self.put(0, 0, at_xy(0, -1), 0, 2)
+            if self.jump:
+                self.put(0, 0, at_xy(0, 2), 0, 3)
 
         def wait(self, hop, piece, count=1):
             landed(self.units * len(self.places) * count, self.sem(hop, piece))
 
         def turn(self):
             self.wait(0, 1)
-            self.put(0, 1, at_xy(0, 1), 0, 3, "first", first_core)
+            if not self.jump:
+                self.put(0, 1, at_xy(0, 1), 0, 3, "first", first_core)
             self.wait(0, 2)
-            self.put(0, 2, at_xy(0, -1), 0, 3, "second", second_core)
+            if not self.jump:
+                self.put(0, 2, at_xy(0, -1), 0, 3, "second", second_core)
 
         def out(self, *pieces):
             for piece in pieces:
@@ -251,20 +300,24 @@
                     self.wait(0, 3)
                 self.put(0, piece, at_xy(1, 0), 1, piece)
                 self.put(0, piece, at_xy(-1, 0), 2, piece)
+                if self.jump and piece in (0, 3):
+                    self.put(0, piece, at_xy(2, 0), 3, piece)
 
         def on(self):
             self.wait(1, 0, 3)
-            for piece in range(3):
+            for piece in range(1 if self.jump else 0, 3):
                 self.put(1, piece, at_xy(1, 0), 3, piece, "first", first_core)
             self.wait(2, 0, 3)
-            for piece in range(3):
+            for piece in range(1 if self.jump else 0, 3):
                 self.put(2, piece, at_xy(-1, 0), 3, piece, "second", second_core)
 
         def on_last(self):
             self.wait(1, 3)
-            self.put(1, 3, at_xy(1, 0), 3, 3, "first", first_core)
+            if not self.jump:
+                self.put(1, 3, at_xy(1, 0), 3, 3, "first", first_core)
             self.wait(2, 3)
-            self.put(2, 3, at_xy(-1, 0), 3, 3, "second", second_core)
+            if not self.jump:
+                self.put(2, 3, at_xy(-1, 0), 3, 3, "second", second_core)
 
         def end(self):
             self.wait(3, 0, 4)
@@ -314,49 +367,49 @@
         def end(self):
             self.wait(self.dx == 2)
 
+    def update_block(buffer, panel):
+        return buffer.at[lax.rem(panel, 2 * Z), panel // (2 * Z)]
+
     def slot(r, c=c):
         return r + (r + 15 - c) // 16 * 16
 
     owner = [z, Z + z]
 
-    g_pin = Gather(0, lambda chip_at, core_at: x_pin.at[chip_at, core_at], 1, "first", cross)
-    g_sum = Gather(1, lambda chip_at, core_at: x_sum.at[chip_at, core_at], 2, "full")
-    g_mid = Gather(2, lambda chip_at, core_at: x_mid.at[chip_at, core_at], 2, "full")
-    g_sel = Gather(3, lambda chip_at, core_at: x_sel.at[chip_at, :, core_at], 4, "full")
+    g_pin = Gather(0, lambda chip_at, core_at: x_pin.at[chip_at, core_at], 1, "both", cross)
+    g_sum = Gather(1, lambda chip_at, core_at: update_block(x_sum, chip_at * 2 + core_at), 2, "both")
+    g_rhs = Gather(5, lambda chip_at, core_at: x_rhs.at[chip_at, core_at], 2, "full")
+    g_mid = Gather(2, lambda chip_at, core_at: x_mid.at[chip_at, core_at], 2, "both")
+    g_sol = Gather(3, lambda chip_at, core_at: x_sol.at[:, chip_at, core_at], 2, "both")
     g_half = Gather(4, lambda chip_at, core_at: x_half.at[lax.rem(chip_at, Z), core_at], 2, "line")
-    f_low = Spread(0, [lambda r: a_low.at[r]], 2)
+    f_low = Spread(0, [lambda r: a_low.at[r]], 2, jump=True)
     f_par = Spread(1, [lambda r: a_par.at[slot(r)]], 4)
     f_piv = Spread(2, [lambda r, j=j: a_piv.at[slot(r, owner[j]), j] for j in range(2)], 1)
     f_up = Spread(3, [lambda r: a_up.at[r]], 2)
-    f_back = Spread(4, [lambda r: a_back.at[r]], 4)
     e_par = Extra(0, a_par.at[16 + c], 4, c)
     e_piv = [Extra(1 + j, a_piv.at[16 + owner[j], j], 1, owner[j]) for j in range(2)]
     extras = [e_par] + e_piv
 
-    x_pin[c, core] = pivot_rhs[y_lo].astype(BF)
-    cross[...] = pivot_rhs[mate_y].astype(BF)
-    a_low[me_r] = lower_update[...]
-    alone = (31 - me_p) // 31 + me_p // 31
-    pl.semaphore_wait(barrier, len(friends) + 2 - alone)
+    landed(4, load_sem.at[1])
+    x_pin[c, core] = pivot_in[y_lo].astype(BF)
+    cross[...] = pivot_in[mate_y].astype(BF)
+    landed(2, load_sem.at[0])
+    pl.semaphore_wait(barrier, len(friends))
 
     f_low.start()
     g_pin.start()
     f_low.out(0)
 
-    is_low, is_high = me_r <= c, me_r >= c
-    a_up[me_r] = upper_update[...]
-    f_up.start()
-    f_up.out(0)
+    landed(15, load_sem.at[2])
 
     @pl.when(is_low)
     def _():
-        a_par[me_r] = parent_lower[...]
-        a_piv[me_r, y_lo] = lower_pivot[y_lo]
+        landed(4, load_sem.at[3])
+        a_piv[me_r, y_lo] = lower_piv_in[y_lo]
 
     @pl.when(is_high)
     def _():
-        a_par[16 + me_r] = parent_upper[...]
-        a_piv[16 + me_r, y_lo] = upper_pivot[y_lo]
+        landed(4, load_sem.at[4])
+        a_piv[16 + me_r, y_lo] = upper_piv_in[y_lo]
 
     @pl.loop(0, 16)
     def _(r):
@@ -381,33 +434,18 @@
     def swap(src, dst, spot, when):
         send(src, dst, 1, h_recv.at[spot], (across, me_r), ("swap", spot), "on", when)
 
-    swap(lower_pivot.at[mate_y], a_piv.at[me_r, y_lo], 2, is_low)
-    swap(upper_pivot.at[mate_y], a_piv.at[16 + me_r, y_lo], 3, is_high)
+    swap(lower_piv_in.at[mate_y], a_piv.at[me_r, y_lo], 2, is_low)
+    swap(upper_piv_in.at[mate_y], a_piv.at[16 + me_r, y_lo], 3, is_high)
 
     start = pl.multiple_of(c * 128, 128)
-    lanes = [maps[:, pl.ds(k * 2048 + start, 128)] - me_p * 128 for k in range(2)]
+    lanes = [maps_in[:, pl.ds(k * 2048 + start, 128)] - me_p * 128 for k in range(2)]
     low = jnp.concatenate([lanes[0][:, :64], lanes[1][:, :64]], axis=1)
     high = jnp.concatenate([lanes[0][:, 64:], lanes[1][:, 64:]], axis=1)
     targets = jnp.where(core == 0, low, high)
     rows = lax.broadcasted_iota(jnp.int32, (128, 128), 0)
     chosen = (rows == targets).astype(F32)
-    pick[...] = chosen.astype(BF)
-    x_sel[c, :, core] = dot(chosen.T.astype(BF), parent_upper[...]).astype(BF).reshape(2, 64, 256)
-
-    g_pin.near()
-    f_low.turn()
-    f_low.out(1, 2)
-    g_pin.far()
-    g_pin.near_over()
-    f_low.out(3)
-    f_low.on()
-    f_up.turn()
-    f_up.out(1, 2)
-    g_sel.start()
-    g_pin.far_over()
-    f_low.on_last()
-    g_pin.all_in()
-    f_low.end()
+    pick[...] = chosen.T.astype(BF)
+    x_rhs[c, core] = parent_in[...].astype(BF)
 
     def square(buffer, r):
         return buffer[r].reshape(128, 128)
@@ -420,20 +458,24 @@
             value += dot(left(r), right(r))
         return value
 
-    value = gemm(update_rhs[...], lambda r: a_low[r], lambda r: square(x_pin, r))
-    u_half[...] = value.astype(BF)
-    for side in range(2):
-        there = goal + side
-        piece = u_half.at[pl.ds(side * 64, 64)]
-        land = moved.at[y_lo]
-        send(piece, land, 1, h_recv.at[y_lo], (there, me_r), ("move", side), "on", there != me_p)
-
-        @pl.when(there == me_p)
-        def _():
-            pltpu.make_async_copy(piece, land, h_recv.at[y_lo]).start()
-
-    g_sel.near()
-    f_up.out(3)
+    g_pin.hop(-2)
+    g_pin.hop(2)
+    f_low.turn()
+    f_low.out(1,2)
+    g_pin.over(-2)
+    g_pin.over(2)
+    f_low.out(3)
+    f_par.start()
+    g_rhs.start()
+    g_pin.hop(-1,1)
+    g_pin.over(0)
+    g_pin.over(-1,1)
+    f_low.on()
+    g_pin.far()
+    f_low.on_last()
+    f_par.out(0)
+    f_par.turn()
+    f_par.out(1,2)
 
     @pl.when(me_r <= mate_c)
     def _():
@@ -444,74 +486,67 @@
         landed(1, h_recv.at[3])
 
     f_piv.start()
-    f_piv.out(0)
-    f_par.start()
-    f_par.out(0)
-    for k in range(2):
-        landed(1, h_recv.at[k])
-
-    total = parent_rhs[...] + dot(pick[...], moved[...].reshape(128, 128))
-    x_sum[c, core] = total.astype(BF)
+    g_pin.all_in()
+    f_low.end()
+    value = gemm(update_in[...], lambda r: a_low[r], lambda r: square(x_pin, r))
+    update_block(x_sum, me_p)[...] = value.astype(BF)
     g_sum.start()
-    g_sel.far()
-    f_up.on()
+    g_rhs.near()
+    f_par.out(3)
+    f_par.on()
     f_piv.turn()
-    f_piv.out(1, 2)
-    g_sum.near()
-    f_par.turn()
-    f_par.out(1, 2)
-    f_piv.out(3)
-    f_up.on_last()
-    g_sel.near_over()
-    g_sum.far()
-    f_par.out(3)
-    f_piv.on()
-    g_sel.far_over()
+    f_piv.out(0,1,2)
     for extra in extras:
         extra.start()
-    g_sum.near_over()
-    f_piv.on_last()
-    f_par.on()
-
-    g_sel.all_in()
-    f_up.end()
-    for k in range(2):
-        value = gemm(
-            jnp.zeros((64, 256), F32), lambda r: a_up[r, k], lambda r: x_sel[r, k].reshape(128, 256)
-        )
-        a_back[me_r, k * 64 : k * 64 + 64] = value.astype(BF)
-    f_back.start()
-    f_back.out(0)
-    g_sum.far_over()
+    g_sum.near()
+    g_rhs.near_over()
+    g_rhs.far()
     f_par.on_last()
-    f_piv.end()
+    f_piv.out(3)
+    for extra in extras:
+        extra.turn()
+    g_sum.far()
+    g_rhs.far_over()
+    f_piv.on()
+    f_up.start()
+    f_par.end()
+    wide = lax.broadcasted_iota(jnp.int32, (256, 128), 0)
+    for r in range(16):
+        for k in range(2):
+            spot = k * 2048 + r * 128
+            chosen = (wide == maps_in[:, spot : spot + 128] - r * 256).astype(F32).astype(BF)
+            a_sum[r, :, k * 128 : k * 128 + 128] = dot(a_par[r], chosen).astype(BF)
+    g_rhs.all_in()
+    acc[...] = gemm(jnp.zeros((128, 128), F32), lambda r: a_par[r], lambda r: pair(x_rhs, r))
     g_sum.all_in()
-    f_par.end()
-
-    value = gemm(jnp.zeros((128, 128), F32), lambda r: a_par[r], lambda r: pair(x_sum, r))
+    value = gemm(acc[...], lambda r: a_sum[r], lambda r: pair(x_sum, r))
     x_mid[c, core] = value.astype(BF)
     g_mid.start()
-
+    for extra in extras:
+        extra.out()
+    f_piv.on_last()
+    f_piv.end()
     value = gemm(jnp.zeros((128, 128), F32), lambda r: square(a_piv, r), lambda r: square(x_pin, r))
     x_half[z, core] = value.astype(BF).reshape(2, 64, 128)
     g_half.start()
-    for extra in extras:
-        extra.turn()
-    f_back.turn()
-    f_back.out(1, 2)
+    f_up.out(0)
+    f_up.turn()
+    f_up.out(1,2)
     g_mid.near()
-    g_half.near()
-    for extra in extras:
-        extra.out()
-    f_back.out(3)
-    g_mid.far()
-    g_half.far()
-    f_back.on()
     for extra in extras:
         extra.on()
-    g_mid.near_over()
+    g_half.near()
+    f_up.out(3)
+    g_mid.far()
     for extra in extras:
         extra.end()
+    g_half.far()
+    f_up.on()
+    g_mid.all_in()
+    value = gemm(jnp.zeros((128, 128), F32), lambda r: a_par[16 + r], lambda r: pair(x_mid, r))
+    x_sol[:, c, core] = dot(pick[...], value.astype(BF)).astype(BF).reshape(2, 64, 128)
+    g_sol.start()
+    parent_out[...] = value
     g_half.all_in()
 
     def half_rows(r):
@@ -520,17 +555,17 @@
     value = gemm(jnp.zeros((128, 128), F32), lambda r: square(a_piv, 16 + r), half_rows)
     direct[...] = value.reshape(2, 64, 128)
     send(direct.at[mate_y], given, 2, h_recv.at[4], (across, me_r), ("swap", 4))
-    f_back.on_last()
-    g_mid.far_over()
-    f_back.end()
+    f_up.on_last()
+    g_sol.near()
+    g_sol.far()
     landed(2, h_recv.at[4])
-    g_mid.all_in()
-
-    parent_out[...] = gemm(jnp.zeros((128, 128), F32), lambda r: a_par[16 + r], lambda r: pair(x_mid, r))
-    value = gemm(jnp.zeros((128, 128), F32), lambda r: a_back[r], lambda r: pair(x_mid, r))
-    child_out[...] = value.reshape(2, 64, 128)
-    child_out[y_lo] += direct[y_lo]
-    child_out[mate_y] += given[...]
+    f_up.end()
+    child_out[y_lo] = direct[y_lo]
+    child_out[mate_y] = given[...]
+    g_sol.all_in()
+    for k in range(2):
+        child_out[k] = gemm(child_out[k], lambda r: a_up[r, k], lambda r: square(x_sol.at[k], r))
+
 
     for spot, units, when in book.values():
 
@@ -553,26 +588,33 @@
             jax.ShapeDtypeStruct((128, 128), F32),
             jax.ShapeDtypeStruct((2, 64, 128), F32),
         ),
-        in_specs=[pl.BlockSpec(memory_space=pltpu.VMEM)] * 10,
+        in_specs=[pl.BlockSpec(memory_space=pltpu.HBM)] * 10,
         out_specs=(pl.BlockSpec(memory_space=pltpu.VMEM),) * 2,
         scratch_shapes=[
             vm((16, 2, 64, 128), BF),
             vm((Z, 2, 2, 64, 128), BF),
-            vm((16, 2, 2, 64, 256), BF),
+            vm((2, 16, 2, 64, 128), BF),
+            vm((16, 2, 128, 128), BF),
             vm((16, 2, 128, 128), BF),
             vm((16, 2, 128, 128), BF),
             vm((16, 128, 128), BF),
             vm((32, 128, 256), BF),
             vm((32, 2, 64, 128), BF),
             vm((16, 2, 64, 128), BF),
+            vm((64, 128), BF),
             vm((16, 128, 256), BF),
-            vm((64, 128), BF),
-            vm((128, 128), BF),
-            vm((2, 64, 128), BF),
+            vm((128, 128), F32),
             vm((64, 128), F32),
             vm((128, 128), BF),
             vm((2, 64, 128), F32),
+            vm((2, 64, 128), F32),
+            vm((128, 128), F32),
+            vm((128, 128), F32),
+            vm((2, 64, 128), BF),
+            vm((2, 64, 128), BF),
+            vm((1, 4096), jnp.int32),
             vm((RULER, 64, 128), BF),
+            dma((5,)),
             dma((N_SEND,)),
             dma((N_GATHER, 12)),
             dma((N_SPREAD, 8)),

time: 81.3 us -> 71.7 us (0.88)
  Pallas kernels: 77.9 us -> 68.7 us
    pallas_call x1, Pallas kernels: 77.9 us -> 68.7 us  [shards(): pl.pallas_call(kernel, out_shape=(jax.ShapeDtypeStruct((128, 128), F32),...]
where the time goes in v4:
time: 71.7 us; the launch traced here: 71.5 us
  Pallas kernels  68.7 us (96%)
  local copies, waits for them, and re-layouts  2.14 us (3%)
    pallas_call x1, Pallas kernels, shards(): pl.pallas_call(kernel, out_shape=(jax.ShapeDtypeStruct((128, 128), F32),...  68.7 us
    unnamed x4, local copies, waits for them, and re-layouts  2.14 us

profile of v4, /device:TPU:1, one launch (start us, length us, event | category | flops | bytes accessed | tf_op | source)
XLA Modules:
  0.0 71.5 jit_solution(323162752203071919)
XLA Ops:
  0.6 68.7 %shard_map.113 = (f32[128,128]{1,0:T(8,128)}, f32[2,64,128]{2,1,0:T(8,128)}) custom-call(f32[2,64,128]{2,1,0:T(8,128)} %pivot_rhs.1, f32[128,128]{1,0:T(8,128)} %update_rhs.1, f32[128,128]{1,0:T(8,128)} %parent_rhs.1, bf16[2,64,128]{2,1,0:T(8,128)(2,1)} %lower_pivot.1, bf16[128,128]{1,0:T(8,128)(2,1)} %lower_update.1, bf16[128,256]{1,0:T(8,128)(2,1)} %parent_lower.1, ...), custom_call_target="tpu_custom_call" | custom-call | tf_op jit(solution)/shard_map/pallas_call | solution.py:585
  69.3 0.0 copy-start
  69.3 1.5 %copy.14 = f32[128,128]{1,0:T(8,128)} copy(f32[128,128]{1,0:T(8,128)} %get-tuple-element.4) | data formatting | bytes 131072
  70.9 0.0 copy-done
  70.9 0.6 copy.15
Async XLA Ops:
  69.3 1.5 %copy-start = (f32[2,64,128]{2,1,0:T(8,128)S(1)}, f32[2,64,128]{2,1,0:T(8,128)}, u32[]{:S(2)}) copy-start(f32[2,64,128]{2,1,0:T(8,128)} %get-tuple-element.5) | copy-start | bytes 196612

commit v5 on v4

--- a/solution.py
+++ b/solution.py
@@ -16,7 +16,7 @@
 HOP = {-2: 0, 2: 1, -1: 2, 1: 2, -3: 3, 3: 3, 4: 4}
 OVER = {0: 5, -2: 6, 2: 7, -1: 8, 1: 8, -3: 9, 3: 9, 4: 10}
 SIBLING = 11
-N_GATHER, N_SPREAD, N_EXTRA, N_SEND = 6, 4, 3, 56
+N_GATHER, N_SPREAD, N_EXTRA, N_SEND = 6, 4, 3, 60
 RULER = 96
 
 
@@ -35,8 +35,7 @@
     upper_pivot,
     upper_update,
     maps,
-    parent_out,
-    child_out,
+    out,
     x_pin,
     x_half,
     x_sol,
@@ -67,6 +66,7 @@
     e_recv,
     h_recv,
 ):
+    parent_out, child_out = out.at[pl.ds(0, 2)], out.at[pl.ds(2, 2)]
     me_p, me_r = lax.axis_index("panel"), lax.axis_index("rhs")
     core = lax.rem(me_p, 2)
     c = me_p // 2
@@ -145,11 +145,24 @@
     odd = jnp.logical_and(second_core, lax.rem(z, 2) == 1)
 
     class Gather:
-        def __init__(self, g, place, units, kind, cross=None):
+        def __init__(self, g, place, units, kind, cross=None, down=False):
             self.g, self.place, self.units, self.kind, self.cross = g, place, units, kind, cross
+            self.down = down
+            self.give = ("give", y_lo == 1) if down else ("all", None)
+            self.take = ("take", y_lo == 0) if down else ("all", None)
+            both = jnp.logical_and
+            low = y_lo == 0
+            self.up_take = ("take first", both(low, first_core)) if down else ("first", first_core)
+            self.down_take = ("take second", both(low, second_core)) if down else ("second", second_core)
+
+        def only(self, action):
+            if self.down:
+                pl.when(y_lo == 0)(action)
+            else:
+                action()
 
         def sem(self, side, col, dist):
-            spot = SIBLING if side else OVER[dist] if col else HOP[dist]
+            spot = SIBLING + col if side else OVER[dist] if col else HOP[dist]
             return g_recv.at[self.g, spot]
 
         def block(self, col, dist, side=0):
@@ -185,7 +198,7 @@
             if self.kind == "both":
                 for d in (2, -2):
                     self.put(0, 0, at_z(d), 0, 0, -d)
-                    self.put(0, 0, beside(d), 0, 1, -d, src=self.cross)
+                    self.put(0, 0, beside(d), 0, 1, -d, *self.give, src=self.cross)
                 for d in (1, -1):
                     self.put(0, 0, at_z(d), 0, 0, -d)
                     if self.cross is not None:
@@ -193,7 +206,7 @@
             else:
                 self.along(0)
             if self.kind != "line":
-                self.put(0, 0, across, 0, 1, 0, src=self.cross)
+                self.put(0, 0, across, 0, 1, 0, *self.give, src=self.cross)
             self.put(0, 0, sib, 1, 0, 0)
 
         def hop(self, *dists):
@@ -203,19 +216,19 @@
                 if self.kind == "full":
                     self.put(0, d, across, 0, 1, d, "first", first_core)
                 if self.kind == "both" and self.cross is None and d in (-1, 1):
-                    self.put(0, d, across, 0, 1, d)
+                    self.put(0, d, across, 0, 1, d, *self.give)
                 self.put(0, d, sib, 1, 0, d)
 
         def over(self, *dists):
-            landed(self.units * len(dists), self.sem(0, 1, dists[0]))
+            self.only(lambda: landed(self.units * len(dists), self.sem(0, 1, dists[0])))
             for d in dists:
                 if self.kind == "both":
-                    self.relay(1, d, ("first", first_core), ("second", second_core))
+                    self.relay(1, d, self.up_take, self.down_take, *self.take)
                 else:
                     if d == 0:
                         self.along(1, "second", second_core)
                     self.relay(1, d, ("even", even), ("odd", odd), "second", second_core)
-                self.put(1, d, sib, 1, 1, d)
+                self.put(1, d, sib, 1, 1, d, *self.take)
 
         def near(self):
             if self.kind == "full":
@@ -251,11 +264,14 @@
             self.over(4)
 
         def all_in(self):
-            landed(self.units * (8 if self.kind == "line" else 16), self.sem(1, 0, 0))
+            landed(self.units * 8, self.sem(1, 0, 0))
+            if self.kind != "line":
+                self.only(lambda: landed(self.units * 8, self.sem(1, 1, 0)))
 
     class Spread:
-        def __init__(self, a, places, units, jump=False):
-            self.a, self.places, self.units, self.jump = a, places, units, jump
+        def __init__(self, a, places, units, jump=False, leap=False):
+            self.a, self.places, self.units = a, places, units
+            self.jump, self.leap = jump, leap
 
         def sem(self, hop, piece):
             spot = {0: piece - 1, 1: 3 + piece // 3, 2: 5 + piece // 3, 3: 7}[hop]
@@ -300,23 +316,23 @@
                     self.wait(0, 3)
                 self.put(0, piece, at_xy(1, 0), 1, piece)
                 self.put(0, piece, at_xy(-1, 0), 2, piece)
-                if self.jump and piece in (0, 3):
+                if self.leap and piece in (0, 3):
                     self.put(0, piece, at_xy(2, 0), 3, piece)
 
         def on(self):
             self.wait(1, 0, 3)
-            for piece in range(1 if self.jump else 0, 3):
+            for piece in range(1 if self.leap else 0, 3):
                 self.put(1, piece, at_xy(1, 0), 3, piece, "first", first_core)
             self.wait(2, 0, 3)
-            for piece in range(1 if self.jump else 0, 3):
+            for piece in range(1 if self.leap else 0, 3):
                 self.put(2, piece, at_xy(-1, 0), 3, piece, "second", second_core)
 
         def on_last(self):
             self.wait(1, 3)
-            if not self.jump:
+            if not self.leap:
                 self.put(1, 3, at_xy(1, 0), 3, 3, "first", first_core)
             self.wait(2, 3)
-            if not self.jump:
+            if not self.leap:
                 self.put(2, 3, at_xy(-1, 0), 3, 3, "second", second_core)
 
         def end(self):
@@ -378,10 +394,10 @@
     g_pin = Gather(0, lambda chip_at, core_at: x_pin.at[chip_at, core_at], 1, "both", cross)
     g_sum = Gather(1, lambda chip_at, core_at: update_block(x_sum, chip_at * 2 + core_at), 2, "both")
     g_rhs = Gather(5, lambda chip_at, core_at: x_rhs.at[chip_at, core_at], 2, "full")
-    g_mid = Gather(2, lambda chip_at, core_at: x_mid.at[chip_at, core_at], 2, "both")
+    g_mid = Gather(2, lambda chip_at, core_at: x_mid.at[chip_at, core_at], 2, "both", down=True)
     g_sol = Gather(3, lambda chip_at, core_at: x_sol.at[:, chip_at, core_at], 2, "both")
     g_half = Gather(4, lambda chip_at, core_at: x_half.at[lax.rem(chip_at, Z), core_at], 2, "line")
-    f_low = Spread(0, [lambda r: a_low.at[r]], 2, jump=True)
+    f_low = Spread(0, [lambda r: a_low.at[r]], 2, jump=True, leap=True)
     f_par = Spread(1, [lambda r: a_par.at[slot(r)]], 4)
     f_piv = Spread(2, [lambda r, j=j: a_piv.at[slot(r, owner[j]), j] for j in range(2)], 1)
     f_up = Spread(3, [lambda r: a_up.at[r]], 2)
@@ -410,6 +426,10 @@
     def _():
         landed(4, load_sem.at[4])
         a_piv[16 + me_r, y_lo] = upper_piv_in[y_lo]
+
+    @pl.when(y_lo == 1)
+    def _():
+        x_mid[:Z] = jnp.zeros((Z, 2, 128, 128), BF)
 
     @pl.loop(0, 16)
     def _(r):
@@ -540,13 +560,13 @@
     g_mid.far()
     for extra in extras:
         extra.end()
-    g_half.far()
     f_up.on()
     g_mid.all_in()
     value = gemm(jnp.zeros((128, 128), F32), lambda r: a_par[16 + r], lambda r: pair(x_mid, r))
     x_sol[:, c, core] = dot(pick[...], value.astype(BF)).astype(BF).reshape(2, 64, 128)
     g_sol.start()
-    parent_out[...] = value
+    parent_out[...] = value.reshape(2, 64, 128)
+    g_half.far()
     g_half.all_in()
 
     def half_rows(r):
@@ -582,14 +602,11 @@
     *arrays, maps = arguments
     vm = pltpu.VMEM
     dma = pltpu.SemaphoreType.DMA
-    return pl.pallas_call(
+    out = pl.pallas_call(
         kernel,
-        out_shape=(
-            jax.ShapeDtypeStruct((128, 128), F32),
-            jax.ShapeDtypeStruct((2, 64, 128), F32),
-        ),
+        out_shape=jax.ShapeDtypeStruct((4, 64, 128), F32),
         in_specs=[pl.BlockSpec(memory_space=pltpu.HBM)] * 10,
-        out_specs=(pl.BlockSpec(memory_space=pltpu.VMEM),) * 2,
+        out_specs=pl.BlockSpec(memory_space=pltpu.VMEM),
         scratch_shapes=[
             vm((16, 2, 64, 128), BF),
             vm((Z, 2, 2, 64, 128), BF),
@@ -616,7 +633,7 @@
             vm((RULER, 64, 128), BF),
             dma((5,)),
             dma((N_SEND,)),
-            dma((N_GATHER, 12)),
+            dma((N_GATHER, 13)),
             dma((N_SPREAD, 8)),
             dma((N_EXTRA,)),
             dma((5,)),
@@ -625,6 +642,7 @@
             collective_id=0, has_side_effects=True, vmem_limit_bytes=60 * 1024 * 1024
         ),
     )(*arrays, maps.reshape(1, -1))
+    return out[:2].reshape(128, 128), out[2:]
 
 
 def solution(mesh):

time: 71.7 us -> 70 us (0.976)
  Pallas kernels: 68.7 us -> 67.6 us
    unnamed x4 -> x0, local copies, waits for them, and re-layouts: 2.14 us -> none
    slice x0 -> x1, local copies, waits for them, and re-layouts: none -> 1.53 us  [shards(): return (out[:2].reshape(128, 128), out[2:])]
    pallas_call x1, Pallas kernels: 68.7 us -> 67.6 us  [shards(): pl.pallas_call(kernel, out_shape=jax.ShapeDtypeStruct((4, 64, 128), F32),...]
where the time goes in v5:
time: 70 us; the launch traced here: 69.8 us
  Pallas kernels  67.6 us (97%)
  local copies, waits for them, and re-layouts  1.53 us (2%)
    pallas_call x1, Pallas kernels, shards(): pl.pallas_call(kernel, out_shape=jax.ShapeDtypeStruct((4, 64, 128), F32),...  67.6 us
    slice x1, local copies, waits for them, and re-layouts, shards(): return (out[:2].reshape(128, 128), out[2:])  1.53 us

profile of v5, /device:TPU:1, one launch (start us, length us, event | category | flops | bytes accessed | tf_op | source)
XLA Modules:
  0.0 69.8 jit_solution(9506812152122215487)
XLA Ops:
  0.6 67.6 %shard_map.113 = f32[4,64,128]{2,1,0:T(8,128)} custom-call(f32[2,64,128]{2,1,0:T(8,128)} %pivot_rhs.1, f32[128,128]{1,0:T(8,128)} %update_rhs.1, f32[128,128]{1,0:T(8,128)} %parent_rhs.1, bf16[2,64,128]{2,1,0:T(8,128)(2,1)} %lower_pivot.1, bf16[128,128]{1,0:T(8,128)(2,1)} %lower_update.1, bf16[128,256]{1,0:T(8,128)(2,1)} %parent_lower.1, ...), custom_call_target="tpu_custom_call" | custom-call | tf_op jit(solution)/shard_map/pallas_call | solution.py:605
  68.3 1.5 %fusion = (f32[2,64,128]{2,1,0:T(8,128)}, f32[2,64,128]{2,1,0:T(8,128)}) fusion(f32[4,64,128]{2,1,0:T(8,128)} %shard_map.113), kind=kLoop, calls=%fused_computation | loop fusion | bytes 262144 | tf_op jit(solution)/shard_map/slice | solution.py:645

commit v6 on v5

--- a/solution.py
+++ b/solution.py
@@ -188,11 +188,11 @@
 
         def relay(self, col, d, up, down, key="all", when=None):
             if d == -2:
+                self.put(col, d, at_z(2), 0, col, 4, *up)
                 self.put(col, d, at_z(1), 0, col, -3, key, when)
-                self.put(col, d, at_z(2), 0, col, 4, *up)
             if d == 2:
+                self.put(col, d, at_z(-2), 0, col, 4, *down)
                 self.put(col, d, at_z(-1), 0, col, 3, key, when)
-                self.put(col, d, at_z(-2), 0, col, 4, *down)
 
         def start(self):
             if self.kind == "both":
@@ -235,10 +235,13 @@
                 self.over(0)
             self.hop(-2)
             self.hop(2)
+            if self.kind == "both" and self.cross is None:
+                self.hop(-1, 1)
             if self.kind == "both":
                 self.over(-2)
                 self.over(2)
-            self.hop(-1, 1)
+            if self.kind != "both" or self.cross is not None:
+                self.hop(-1, 1)
             if self.kind == "both":
                 self.over(0)
                 if self.cross is not None:
@@ -525,8 +528,8 @@
     f_piv.out(3)
     for extra in extras:
         extra.turn()
+    g_rhs.far_over()
     g_sum.far()
-    g_rhs.far_over()
     f_piv.on()
     f_up.start()
     f_par.end()
@@ -545,17 +548,16 @@
     for extra in extras:
         extra.out()
     f_piv.on_last()
+    f_up.out(0)
+    f_up.turn()
+    f_up.out(1,2)
+    g_mid.near()
     f_piv.end()
     value = gemm(jnp.zeros((128, 128), F32), lambda r: square(a_piv, r), lambda r: square(x_pin, r))
     x_half[z, core] = value.astype(BF).reshape(2, 64, 128)
     g_half.start()
-    f_up.out(0)
-    f_up.turn()
-    f_up.out(1,2)
-    g_mid.near()
     for extra in extras:
         extra.on()
-    g_half.near()
     f_up.out(3)
     g_mid.far()
     for extra in extras:
@@ -566,6 +568,9 @@
     x_sol[:, c, core] = dot(pick[...], value.astype(BF)).astype(BF).reshape(2, 64, 128)
     g_sol.start()
     parent_out[...] = value.reshape(2, 64, 128)
+    g_half.near()
+    f_up.on_last()
+    g_sol.near()
     g_half.far()
     g_half.all_in()
 
@@ -575,8 +580,6 @@
     value = gemm(jnp.zeros((128, 128), F32), lambda r: square(a_piv, 16 + r), half_rows)
     direct[...] = value.reshape(2, 64, 128)
     send(direct.at[mate_y], given, 2, h_recv.at[4], (across, me_r), ("swap", 4))
-    f_up.on_last()
-    g_sol.near()
     g_sol.far()
     landed(2, h_recv.at[4])
     f_up.end()

time: 70 us -> 69.4 us (level)
  no operation moved by 1% of the time
where the time goes in v6:
time: 69.4 us; the launch traced here: 69.2 us
  Pallas kernels  67 us (97%)
  local copies, waits for them, and re-layouts  1.53 us (2%)
    pallas_call x1, Pallas kernels, shards(): pl.pallas_call(kernel, out_shape=jax.ShapeDtypeStruct((4, 64, 128), F32),...  67 us
    slice x1, local copies, waits for them, and re-layouts, shards(): return (out[:2].reshape(128, 128), out[2:])  1.53 us

profile of v6, /device:TPU:1, one launch (start us, length us, event | category | flops | bytes accessed | tf_op | source)
XLA Modules:
  0.0 69.2 jit_solution(13092156618562515072)
XLA Ops:
  0.6 67.0 %shard_map.113 = f32[4,64,128]{2,1,0:T(8,128)} custom-call(f32[2,64,128]{2,1,0:T(8,128)} %pivot_rhs.1, f32[128,128]{1,0:T(8,128)} %update_rhs.1, f32[128,128]{1,0:T(8,128)} %parent_rhs.1, bf16[2,64,128]{2,1,0:T(8,128)(2,1)} %lower_pivot.1, bf16[128,128]{1,0:T(8,128)(2,1)} %lower_update.1, bf16[128,256]{1,0:T(8,128)(2,1)} %parent_lower.1, ...), custom_call_target="tpu_custom_call" | custom-call | tf_op jit(solution)/shard_map/pallas_call | solution.py:608
  67.7 1.5 %fusion = (f32[2,64,128]{2,1,0:T(8,128)}, f32[2,64,128]{2,1,0:T(8,128)}) fusion(f32[4,64,128]{2,1,0:T(8,128)} %shard_map.113), kind=kLoop, calls=%fused_computation | loop fusion | bytes 262144 | tf_op jit(solution)/shard_map/slice | solution.py:648
